TPU v7x, 32 devices: a whole 2x2x4 slice. The times are simulated.
32 devices in a mesh: orient: 8 (over z, y), dom: 4 (over x, core).
Axes of the slice: x: 2, y: 2, z: 4, core: 2. Of those that a mesh axis runs over, the one named last changes fastest.
Arguments:
- particles: bfloat16 [256, 8448], P(('dom', 'orient')), parts along dimension 0, may hold values from -12 to 12
- defocus: float32 [256], P(('dom', 'orient')), parts along dimension 0, may hold values from 10 to 60
- inv_noise: float32 [4224], replicated, may hold values from 0.5 to 2
- references: bfloat16 [13824, 8448], P(('dom', 'orient')), parts along dimension 0, may hold values from -0.25 to 0.25
- thresholds: int32 [256], P('dom'), parts along dimension 0, may hold values from 512 to 1023
- range_start: int32 [256], P('dom'), parts along dimension 0, may hold values from 0 to 3455
- range_len: int32 [256], P('dom'), parts along dimension 0, may hold values from 36 to 1727
Outputs:
- posterior: float32 [256, 3456], P('dom', 'orient'), parts along dimension 0
- cumulative: float32 [256, 3456], P('dom', 'orient'), parts along dimension 0
- log_evidence: float32 [256], P('dom'), parts along dimension 0
- kept_mass: float32 [256], P('dom'), parts along dimension 0
There are 4 independent parts, one for each index of `dom`. A program takes and returns all parts, laid end to end along the dimension named above; an argument that names none is the same for every part. Nothing has to cross between parts.
All inputs are finite; a program needn't handle non-finite values.
Results may differ from a plain program's by a relative error of at most 0.0004.
The roundings to bfloat16 on the way count: a program that leaves them out, or rounds other values in their place, can miss the bound.
Values may be sent and summed in bfloat16 or wider, within the bound.
No kernel may reach another device: no remote copies, remote signals or barrier semaphores. Data moves between devices by JAX's collectives and lax.ppermute only.
A program may use at most 64 MiB of HBM per device.

v0:
```python
import math

import jax
import jax.numpy as jnp
from jax import lax
from jax.sharding import PartitionSpec as P


def ctf_table(defocus, coef):
    index = jnp.arange(coef, dtype=jnp.int32)
    row_pos = (index // 128).astype(jnp.float32)
    col_pos = (index % 128 - 64).astype(jnp.float32)
    freq = math.pi * (row_pos * row_pos + col_pos * col_pos) / 16384.0
    return -jnp.sin(defocus[:, None] * freq[None, :] + 0.07)


def on_device(particles, defocus, inv_noise, references, thresholds, range_start, range_len):
    coef = inv_noise.shape[0]
    feat = 2 * coef
    ori_dev = references.shape[0]
    ctf = ctf_table(defocus, coef)
    ctf_both = jnp.concatenate([ctf, ctf], axis=1)
    noise_both = jnp.concatenate([inv_noise, inv_noise])
    weighted = (particles.astype(jnp.float32) * ctf_both * noise_both[None, :]).astype(jnp.bfloat16)
    ctf_power = (ctf * ctf * inv_noise[None, :]).astype(jnp.bfloat16)
    packed = jnp.concatenate([weighted, ctf_power], axis=1)
    real_part = references[:, :coef].astype(jnp.float32)
    imag_part = references[:, coef:].astype(jnp.float32)
    power = (real_part * real_part + imag_part * imag_part).astype(jnp.bfloat16)
    dims = (((1,), (1,)), ((), ()))
    piece = lax.all_gather(packed, "orient", axis=0, tiled=True)
    cross = lax.dot_general(piece[:, :feat], references, dims, preferred_element_type=jnp.float32)
    energy = lax.dot_general(piece[:, feat:], power, dims, preferred_element_type=jnp.float32)
    scores = cross - 0.5 * energy
    local_top = jnp.max(scores, axis=1)
    local_sum = jnp.sum(jnp.exp(scores - local_top[:, None]), axis=1)
    all_tops, all_sums = (
        lax.all_gather(local_top[None, :], "orient", axis=0, tiled=True),
        lax.all_gather(local_sum[None, :], "orient", axis=0, tiled=True),
    )
    top_score = jnp.max(all_tops, axis=0)
    scaled = all_sums * jnp.exp(all_tops - top_score[None, :])
    total = jnp.sum(scaled, axis=0)
    ranks = jnp.arange(all_tops.shape[0], dtype=jnp.int32)
    earlier_rows = (ranks < lax.axis_index("orient"))[:, None]
    shifted = jnp.sum(jnp.where(earlier_rows, scaled, 0.0), axis=0)
    expon = jnp.exp(scores - top_score[:, None])
    posterior = expon / total[:, None]
    row_ids = lax.broadcasted_iota(jnp.int32, (ori_dev, ori_dev), 0)
    col_ids = lax.broadcasted_iota(jnp.int32, (ori_dev, ori_dev), 1)
    upper = (row_ids <= col_ids).astype(jnp.float32)
    running = jnp.dot(
        expon, upper, precision=lax.Precision.HIGHEST, preferred_element_type=jnp.float32
    )
    cumulative = (shifted[:, None] + running) / total[:, None]
    before = cumulative - posterior
    fraction = thresholds.astype(jnp.float32) / 1024.0
    kept = jnp.minimum(jnp.maximum(fraction[:, None] - before, 0.0), posterior)
    all_orients = lax.axis_size("orient") * ori_dev
    orient_ids = lax.axis_index("orient") * ori_dev + jnp.arange(ori_dev, dtype=jnp.int32)
    inside = (orient_ids[None, :] - range_start[:, None]) % all_orients < range_len[:, None]
    local_kept = jnp.sum(jnp.where(inside, kept, 0.0), axis=1)
    kept_mass = lax.psum(local_kept, "orient")
    log_evidence = top_score + jnp.log(total)
    return (posterior, cumulative, log_evidence, kept_mass)


def solution(mesh):
    return jax.shard_map(
        on_device,
        mesh=mesh,
        in_specs=(
            P(("dom", "orient"), None),
            P(("dom", "orient")),
            P(),
            P(("dom", "orient"), None),
            P("dom"),
            P("dom"),
            P("dom"),
        ),
        out_specs=(P("dom", "orient"), P("dom", "orient"), P("dom"), P("dom")),
        check_vma=False,
    )
```

profile of v0, /device:TPU:0, one launch (start us, length us, event | category | flops | bytes accessed | tf_op | source)
XLA Modules:
  0.0 113.0 jit_solution(12283271416409016182)
XLA Ops:
  7.2 0.0 all-gather.4.cloned.1.call-start
  7.2 0.8 pad_maximum_fusion.1
  8.0 1.3 %fusion.7 = (f32[8,4224]{1,0:T(8,128)S(1)}, bf16[8,4224]{1,0:T(8,128)(2,1)S(1)}) fusion(f32[4224]{0:T(1024)S(1)} %fusion.23, f32[8]{0:T(128)} %param.8, f32[4224]{0:T(1024)} %param.9), kind=kLoop, calls=%fused_computation.16 | loop fusion | flops 202752 | bytes 236576 | tf_op jit(solution)/shard_map/neg | solution.py:14
  9.3 1.0 fusion.6
  10.3 0.7 pad_maximum_fusion
  11.0 0.0 all-gather.4.cloned.1.call-update
  11.0 1.2 %dynamic-slice = u32[1]{0:T(128)} dynamic-slice(u32[32]{0:T(128)} %constant.75, u32[]{:T(128)S(6)} %add.76), dynamic_slice_sizes={1} | dynamic-slice | bytes 12
  12.9 0.7 convert_multiply_fusion
  13.6 45.1 %all-gather.4.cloned.1.call-done = bf16[64,12672]{1,0:T(8,128)(2,1)} async-done(((bf16[8,12672]{1,0:T(8,128)(2,1)}), bf16[64,12672]{1,0:T(8,128)(2,1)}) %all-gather.4.cloned.1.call-update) | async-done | bytes 1622032 | tf_op jit(solution)/shard_map/all_gather | solution.py:31
  58.7 5.0 %fusion.2 = f32[64,432]{1,0:T(8,128)S(1)} fusion(bf16[432,8448]{1,0:T(8,128)(2,1)} %param.10, bf16[64,12672]{1,0:T(8,128)(2,1)} %all-gather.4.cloned.1.call-done), kind=kOutput, calls=%fused_computation.5 | convolution fusion | flops 244546560 | bytes 7950336 | tf_op jit(solution)/shard_map/dot_general | solution.py:33
  63.6 0.4 copy-done
  64.0 0.4 copy-done.1
  64.5 2.3 %fusion.30 = (f32[64]{0:T(128)S(1)}, f32[64,432]{1,0:T(8,128)S(1)}) fusion(f32[64,432]{1,0:T(8,128)S(1)} %fusion.2, bf16[432,8448]{1,0:T(8,128)(2,1)S(1)} %copy-done, bf16[64,12672]{1,0:T(8,128)(2,1)S(1)} %copy-done.1), kind=kOutput, calls=%fused_computation.53 | convolution fusion | flops 467195840 | bytes 8622336 | tf_op jit(solution)/shard_map/dot_general | solution.py:32
  66.8 0.2 exponential_reduce_fusion
  67.0 0.2 dynamic-update-slice
  67.2 0.2 dynamic-update-slice.1
  67.4 18.8 %all-reduce.2 = (f32[512]{0:T(512)S(1)}, f32[512]{0:T(512)S(1)}) all-reduce(f32[512]{0:T(512)S(1)} %dynamic-update-slice.1, f32[512]{0:T(512)S(1)} %dynamic-update-slice), channel_id=3, replica_groups=mesh['orient'=8,'dom'=4] {'orient'}, use_global_device_ids=true, to_apply=%add.1 | all-reduce | flops 1024 | bytes 8192
  86.2 0.1 reshape.54
  86.3 0.1 reshape.55
  86.4 0.1 select_reduce_fusion.1
  86.4 0.5 log_add_fusion
  87.0 0.0 copy-done.2
  87.0 1.2 %select_reduce_fusion = (f32[64]{0:T(128)S(1)}, f32[64,432]{1,0:T(8,128)}, f32[64,432]{1,0:T(8,128)}) fusion(f32[64]{0:T(128)S(1)} %convert_multiply_fusion, s32[64]{0:T(128)S(1)} %copy-done.2, s32[64]{0:T(128)S(1)} %copy-done.3, s32[432]{0:T(512)S(1)} %iota_add_fusion, f32[64]{0:T(128)S(1)} %get-tuple-element.5, f32[64,432]{1,0:T(8,128)S(1)} %get-tuple-element.13, ...), kind=kOutput, calls=%fused_computation.18 | convolution fusion | flops 144039104 | bytes 335296 | tf_op jit(solution)/shard_map/dot_general | solution.py:52
  88.1 18.0 %psum.7 = f32[64]{0:T(128)} all-reduce(f32[64]{0:T(128)S(1)} %get-tuple-element.8), channel_id=1, replica_groups=mesh['orient'=8,'dom'=4] {'orient'}, use_global_device_ids=true, to_apply=%region_6.7 | all-reduce | flops 64 | bytes 512 | tf_op jit(solution)/shard_map/psum | solution.py:63
  (11 shorter events, 0.1 us)
Async XLA Ops:
  7.2 51.5 %all-gather.4.cloned.1.call-start = ((), (), s32[]{:S(2)}) async-start(), calls=%async_computation | async-start | bytes 1824768 | tf_op jit(solution)/shard_map/all_gather | solution.py:31
  58.6 5.4 %copy-start = (bf16[432,8448]{1,0:T(8,128)(2,1)S(1)}, bf16[432,8448]{1,0:T(8,128)(2,1)}, u32[]{:S(2)}) copy-start(bf16[432,8448]{1,0:T(8,128)(2,1)} %param.10) | copy-start | bytes 21897220
  58.7 5.8 %copy-start.1 = (bf16[64,12672]{1,0:T(8,128)(2,1)S(1)}, bf16[64,12672]{1,0:T(8,128)(2,1)}, u32[]{:S(2)}) copy-start(bf16[64,12672]{1,0:T(8,128)(2,1)} %all-gather.4.cloned.1.call-done) | copy-start | bytes 4866052
  64.4 22.5 %copy-start.2 = (s32[64]{0:T(128)S(1)}, s32[64]{0:T(128)}, u32[]{:S(2)}) copy-start(s32[64]{0:T(128)} %param.13) | copy-start | bytes 772
  64.4 22.5 %copy-start.3 = (s32[64]{0:T(128)S(1)}, s32[64]{0:T(128)}, u32[]{:S(2)}) copy-start(s32[64]{0:T(128)} %param.12) | copy-start | bytes 772
Sparse Core Ops, SparseCore 0:
  11.1 47.4 all-gather.3
where the time goes:
time: 113 us
  waiting for transfers between devices  45.1 us (40%)
  blocking collectives  36.7 us (32%)
  between operations  14.7 us (13%)
  matrix products  8.47 us (7%)
  other arithmetic  5.25 us (5%)
  local copies, waits for them, and re-layouts  2.66 us (2%)
    all_gather x1, waiting for transfers between devices, on_device(): piece = lax.all_gather(packed, 'orient', axis=0, tiled=True)  45.1 us
    unnamed x1, blocking collectives  18.8 us
    psum x1, blocking collectives, on_device(): kept_mass = lax.psum(local_kept, 'orient')  18 us
    dot_general x1, matrix products, on_device(): lax.dot_general(piece[:, feat:], power, dims, preferred_element_type=jnp....  4.98 us
    unnamed x13, local copies, waits for them, and re-layouts  2.51 us
    dot_general x1, matrix products, on_device(): lax.dot_general(piece[:, :feat], references, dims, preferred_element_type...  2.33 us
  transfers between devices with their start and end apart: 1, of which 1 were waited for; matrix products, arithmetic and copies ran while one was open for 2% of the time, Pallas kernels for 0%

commit v1 on v0

v1 whole, which is shorter than its diff:
```python
import math

import jax
import jax.numpy as jnp
from jax import lax
from jax.experimental import pallas as pl
from jax.experimental.pallas import tpu as pltpu
from jax.sharding import PartitionSpec as P

LANES = 128
VMEM = pl.BlockSpec(memory_space=pltpu.VMEM)
SMEM = pl.BlockSpec(memory_space=pltpu.SMEM)
HBM = pl.BlockSpec(memory_space=pl.ANY)


def sine(x):
    turns = jnp.floor(x * (1.0 / math.pi) + 0.5)
    rest = x - turns * 3.1414794921875
    rest = rest - turns * 0.00011315941810607910156
    rest = rest - turns * 1.9841872589410058936e-09
    sq = rest * rest
    poly = sq * 2.6083159809786593541503e-06 - 0.0001981069071916863322258
    poly = poly * sq + 0.00833307858556509017944336
    poly = poly * sq - 0.166666597127914428710938
    value = rest + rest * (sq * poly)
    half = turns * 0.5
    odd = half - jnp.floor(half)
    return value * (1.0 - 4.0 * odd)


def column(row):
    size = row.shape[1]
    down = lax.broadcasted_iota(jnp.int32, (size, size), 0)
    across = lax.broadcasted_iota(jnp.int32, (size, size), 1)
    return jnp.sum(jnp.where(down == across, row, 0.0), axis=1, keepdims=True)


def pack_body(particles, defocus, out, sem):
    feat = particles.shape[1]
    copy = pltpu.make_async_copy(particles, out.at[:, pl.ds(0, feat)], sem)
    copy.start()
    value = column(defocus[...])
    high = value.astype(jnp.bfloat16).astype(jnp.float32)
    mid = (value - high).astype(jnp.bfloat16).astype(jnp.float32)
    low = value - high - mid
    lane = lax.broadcasted_iota(jnp.int32, (value.shape[0], LANES), 1)
    parts = jnp.where(lane == 0, high, jnp.where(lane == 1, mid, jnp.where(lane == 2, low, 0.0)))
    out[:, pl.ds(feat, LANES)] = parts.astype(jnp.bfloat16)
    copy.wait()


def power_body(references, out):
    rows, coef = out.shape
    for k in range(0, coef, LANES):
        real = references[:, pl.ds(k, LANES)].astype(jnp.float32)
        imag = references[:, pl.ds(coef + k, LANES)].astype(jnp.float32)
        out[:, pl.ds(k, LANES)] = (real * real + imag * imag).astype(jnp.bfloat16)


def score_body(*refs, count, all_orients):
    shard, start, length, noise, references, power = refs[:6]
    pieces = refs[6 : 6 + count]
    scores, stats = refs[6 + count : 8 + count]
    stage, focus, weighted, energy = refs[8 + count :]
    rows = pieces[0].shape[0]
    ori, feat = references.shape
    coef = feat // 2
    me = shard[0]
    places = [pl.ds(pl.multiple_of((me ^ b) * rows, rows), rows) for b in range(count)]
    for b in range(count):
        bits = pieces[b][:, pl.ds(feat, LANES)].astype(jnp.float32)
        value = bits[:, 0:1] + bits[:, 1:2] + bits[:, 2:3]
        focus[places[b], :] = jnp.broadcast_to(value, (rows, LANES))
    dims = (((1,), (1,)), ((), ()))
    total = None
    for first in range(0, coef, 2 * LANES):
        width = min(2 * LANES, coef - first)
        for k in range(first, first + width, LANES):
            at = pl.ds(k, LANES)
            also = pl.ds(coef + k, LANES)
            for b in range(count):
                stage[places[b], at] = pieces[b][:, at].astype(jnp.float32)
                stage[places[b], also] = pieces[b][:, also].astype(jnp.float32)
            row_pos = float(k // 128)
            col_pos = (lax.broadcasted_iota(jnp.int32, (1, LANES), 1) - 64).astype(jnp.float32)
            freq = math.pi * (row_pos * row_pos + col_pos * col_pos) / 16384.0
            ctf = -sine(focus[...] * freq + 0.07)
            noise_row = noise[:, at]
            weighted[:, at] = (stage[:, at] * ctf * noise_row).astype(jnp.bfloat16)
            weighted[:, also] = (stage[:, also] * ctf * noise_row).astype(jnp.bfloat16)
            energy[:, at] = (-0.5 * (ctf * ctf * noise_row).astype(jnp.bfloat16).astype(jnp.float32)).astype(jnp.bfloat16)
        for left, right, k in (
            (references, weighted, first),
            (references, weighted, coef + first),
            (power, energy, first),
        ):
            at = pl.ds(k, width)
            part = lax.dot_general(left[:, at], right[:, at], dims, preferred_element_type=jnp.float32)
            total = part if total is None else total + part
    scores[...] = total
    top = jnp.max(total, axis=0, keepdims=True)
    expon = jnp.exp(total - top)
    index = me * ori + lax.broadcasted_iota(jnp.int32, total.shape, 0)
    begin = start[...]
    end = begin + length[...]
    end = jnp.where(end > all_orients, end - all_orients, end)
    stats[0:1, :] = top
    stats[1:2, :] = jnp.sum(expon, axis=0, keepdims=True)
    stats[2:3, :] = jnp.sum(jnp.where(index < begin, expon, 0.0), axis=0, keepdims=True)
    stats[3:4, :] = jnp.sum(jnp.where(index < end, expon, 0.0), axis=0, keepdims=True)


def running_body(scores, stats, expon_out, running_out, expon_pad, running_pad):
    ori, count = scores.shape
    top = stats[0:1, :]
    carry = jnp.zeros((1, count), jnp.float32)
    sub = lax.broadcasted_iota(jnp.int32, (8, count), 0)
    for o in range(0, ori, 8):
        value = jnp.exp(scores[pl.ds(o, 8), :] - top)
        total = value
        for step in (1, 2, 4):
            total = total + jnp.where(sub >= step, pltpu.roll(total, step, 0), 0.0)
        total = total + carry
        carry = total[7:8, :]
        expon_pad[pl.ds(o, 8), pl.ds(0, count)] = value
        running_pad[pl.ds(o, 8), pl.ds(0, count)] = total
    for o in range(0, ori, LANES):
        width = min(LANES, ori - o)
        for c in range(0, count, LANES):
            high = min(LANES, count - c)
            for pad, out in ((expon_pad, expon_out), (running_pad, running_out)):
                block = pad[pl.ds(o, LANES), pl.ds(c, LANES)].T
                out[pl.ds(c, high), pl.ds(o, width)] = block[:high, :width]


def final_body(shard, near, far, thresholds, start, length, expon, running, *outs, all_orients):
    posterior, cumulative, evidence, mass = outs
    me = shard[0]
    half = near.shape[0] // 4
    tables = [near[pl.ds(4 * b, 4), :] for b in range(half)] + [far[pl.ds(4 * b, 4), :] for b in range(half)]
    top = tables[0][0:1, :]
    for table in tables[1:]:
        top = jnp.maximum(top, table[0:1, :])
    sums = jnp.zeros_like(tables[0])
    shifted = jnp.zeros_like(top)
    for b, table in enumerate(tables):
        scaled = table * jnp.exp(table[0:1, :] - top)
        sums = sums + scaled
        earlier = jnp.where((me ^ b) < me, 1.0, 0.0)
        shifted = shifted + earlier * scaled[1:2, :]
    total = sums[1:2, :]
    evidence[...] = top + jnp.log(total)
    fraction = thresholds[...].astype(jnp.float32) / 1024.0
    wraps = start[...] + length[...] > all_orients
    before = jnp.minimum(sums[2:3, :] / total, fraction)
    until = jnp.minimum(sums[3:4, :] / total, fraction)
    whole = jnp.where(wraps, jnp.minimum(1.0, fraction), 0.0)
    mass[...] = until - before + whole
    scale = column(jnp.exp(tables[0][0:1, :] - top) / total)
    shift = column(shifted / total)
    posterior[...] = expon[...] * scale
    cumulative[...] = running[...] * scale + shift


def on_device(particles, defocus, inv_noise, references, thresholds, range_start, range_len):
    n = lax.axis_size("orient")
    rows, feat = particles.shape
    coef = inv_noise.shape[0]
    ori = references.shape[0]
    count = n * rows
    all_orients = n * ori
    shard = lax.axis_index("orient").astype(jnp.int32).reshape(1)
    start = range_start.reshape(1, count)
    length = range_len.reshape(1, count)
    f32, bf16 = jnp.float32, jnp.bfloat16

    def swap(x, b):
        return lax.ppermute(x, "orient", [(i, i ^ b) for i in range(n)])

    packed = pl.pallas_call(
        pack_body,
        name="pack",
        out_shape=jax.ShapeDtypeStruct((rows, feat + LANES), bf16),
        in_specs=[HBM, VMEM],
        out_specs=VMEM,
        scratch_shapes=[pltpu.SemaphoreType.DMA],
    )(particles, defocus.reshape(1, rows))

    half = n // 2
    pieces = {0: packed, half: swap(packed, half)}
    for source in (0, half):
        for b in range(half - 1, 0, -1):
            pieces[source ^ b] = swap(pieces[source], b)

    power = pl.pallas_call(
        power_body,
        name="power",
        out_shape=jax.ShapeDtypeStruct((ori, coef), bf16),
        in_specs=[VMEM],
        out_specs=VMEM,
    )(references)

    scores, stats = pl.pallas_call(
        lambda *refs: score_body(*refs, count=n, all_orients=all_orients),
        name="score",
        out_shape=(jax.ShapeDtypeStruct((ori, count), f32), jax.ShapeDtypeStruct((4, count), f32)),
        in_specs=[SMEM] + [VMEM] * (5 + n),
        out_specs=(VMEM, VMEM),
        scratch_shapes=[
            pltpu.VMEM((count, feat), f32),
            pltpu.VMEM((count, LANES), f32),
            pltpu.VMEM((count, feat), bf16),
            pltpu.VMEM((count, coef), bf16),
        ],
    )(shard, start, length, inv_noise.reshape(1, coef), references, power, *[pieces[b] for b in range(n)])

    near = stats
    b = 1
    while b < half:
        near = jnp.concatenate([near, swap(near, b)], axis=0)
        b *= 2
    far = swap(near, half)

    pad_ori = -(-ori // LANES) * LANES
    pad_count = -(-count // LANES) * LANES
    expon, running = pl.pallas_call(
        running_body,
        name="running",
        out_shape=(jax.ShapeDtypeStruct((count, ori), f32),) * 2,
        in_specs=[VMEM, VMEM],
        out_specs=(VMEM, VMEM),
        scratch_shapes=[pltpu.VMEM((pad_ori, pad_count), f32)] * 2,
    )(scores, stats)

    posterior, cumulative, evidence, mass = pl.pallas_call(
        lambda *refs: final_body(*refs, all_orients=all_orients),
        name="final",
        out_shape=(jax.ShapeDtypeStruct((count, ori), f32),) * 2 + (jax.ShapeDtypeStruct((1, count), f32),) * 2,
        in_specs=[SMEM] + [VMEM] * 7,
        out_specs=(VMEM,) * 4,
    )(shard, near, far, thresholds.reshape(1, count), start, length, expon, running)
    return posterior, cumulative, evidence.reshape(count), mass.reshape(count)


def solution(mesh):
    return jax.shard_map(
        on_device,
        mesh=mesh,
        in_specs=(
            P(("dom", "orient"), None),
            P(("dom", "orient")),
            P(),
            P(("dom", "orient"), None),
            P("dom"),
            P("dom"),
            P("dom"),
        ),
        out_specs=(P("dom", "orient"), P("dom", "orient"), P("dom"), P("dom")),
        check_vma=False,
    )
```

time: 113 us -> 50.8 us (0.45)
  blocking collectives: 36.7 us -> 0 us
  waiting for transfers between devices: 45.1 us -> 9.42 us
  Pallas kernels: 0 us -> 20.8 us
  starting transfers between devices: 0.04 us -> 15.4 us
  between operations: 14.7 us -> 0.73 us
  matrix products: 8.47 us -> 0 us
  other arithmetic: 5.25 us -> 1.38 us
    all_gather x1 -> x0, waiting for transfers between devices: 45.1 us -> none  [on_device(): piece = lax.all_gather(packed, 'orient', axis=0, tiled=True)]
    pallas_call x0 -> x5, Pallas kernels: none -> 20.8 us  [the longest x1 8.6 us: on_device(): pl.pallas_call(lambda *refs: score_body(*refs, count=n, all_orients=all_o...]
    unnamed x1 -> x0, blocking collectives: 18.8 us -> none
    psum x1 -> x0, blocking collectives: 18 us -> none  [on_device(): kept_mass = lax.psum(local_kept, 'orient')]
    ppermute x0 -> x10, starting transfers between devices: none -> 15.4 us  [swap(): return lax.ppermute(x, 'orient', [(i, i ^ b) for i in range(n)])]
    ppermute x0 -> x10, waiting for transfers between devices: none -> 9.42 us  [swap(): return lax.ppermute(x, 'orient', [(i, i ^ b) for i in range(n)])]
    dot_general x3 -> x0, matrix products: 8.47 us -> none  [the longest x1 4.98 us: on_device(): lax.dot_general(piece[:, feat:], power, dims, preferred_element_type=jnp....]
    reshape x0 -> x1, local copies, waits for them, and re-layouts: none -> 1.34 us  [on_device(): inv_noise.reshape(1, coef)]
  transfers between devices with their start and end apart: 1 -> 10, of which waited for: 1 -> 4; matrix products, arithmetic and copies ran while one was open for 2% -> 3% of each run, Pallas kernels for 0% -> 16%
where the time goes in v1:
time: 50.8 us; the launch traced here: 50.4 us
  Pallas kernels  20.8 us (41%)
  starting transfers between devices  15.4 us (30%)
  waiting for transfers between devices  9.42 us (19%)
  local copies, waits for them, and re-layouts  2.71 us (5%)
  other arithmetic  1.38 us (3%)
  between operations  0.73 us (1%)
    ppermute x10, starting transfers between devices, swap(): return lax.ppermute(x, 'orient', [(i, i ^ b) for i in range(n)])  15.4 us
    ppermute x10, waiting for transfers between devices, swap(): return lax.ppermute(x, 'orient', [(i, i ^ b) for i in range(n)])  9.42 us
    pallas_call x1, Pallas kernels, on_device(): pl.pallas_call(lambda *refs: score_body(*refs, count=n, all_orients=all_o...  8.6 us
    pallas_call x1, Pallas kernels, on_device(): pl.pallas_call(power_body, name='power', out_shape=jax.ShapeDtypeStruct((...  6.25 us
    pallas_call x1, Pallas kernels, on_device(): pl.pallas_call(pack_body, name='pack', out_shape=jax.ShapeDtypeStruct((ro...  2.22 us
    pallas_call x1, Pallas kernels, on_device(): pl.pallas_call(lambda *refs: final_body(*refs, all_orients=all_orients),...  1.88 us
    pallas_call x1, Pallas kernels, on_device(): pl.pallas_call(running_body, name='running', out_shape=(jax.ShapeDtypeStr...  1.88 us
    concatenate x2, other arithmetic, on_device(): near = jnp.concatenate([near, swap(near, b)], axis=0)  1.38 us
  transfers between devices with their start and end apart: 10, of which 4 were waited for; matrix products, arithmetic and copies ran while one was open for 3% of the time, Pallas kernels for 16%

profile of v1, /device:TPU:0, one launch (start us, length us, event | category | flops | bytes accessed | tf_op | source)
XLA Modules:
  0.0 50.4 jit_solution(4984170366050347381)
XLA Ops:
  0.6 2.2 %pack.1.refs_6_ = bf16[8,8576]{1,0:T(8,128)(2,1)} custom-call(bf16[8,8448]{1,0:T(8,128)(2,1)} %particles.1, f32[1,8]{1,0:T(1,128)} %bitcast.11), custom_call_target="tpu_custom_call" | custom-call | tf_op jit(solution)/shard_map/pack/pallas_call | solution.py:180
  2.9 4.1 %collective-permute-start.3 = (bf16[8,8576]{1,0:T(8,128)(2,1)}, bf16[8,8576]{1,0:T(8,128)(2,1)S(1)}, u32[]{:S(2)}, u32[]{:S(2)}) collective-permute-start(bf16[8,8576]{1,0:T(8,128)(2,1)} %pack.1.refs_6_), channel_id=1, source_target_pairs={{0,16},{4,20},{8,24},{12,28},{16,0},{20,4},{24,8},{28,12},{1,17},{... | collective-permute-start | bytes 411656 | tf_op jit(solution)/shard_map/ppermute | solution.py:178
  7.0 2.5 %collective-permute-start.2 = (bf16[8,8576]{1,0:T(8,128)(2,1)}, bf16[8,8576]{1,0:T(8,128)(2,1)S(1)}, u32[]{:S(2)}, u32[]{:S(2)}) collective-permute-start(bf16[8,8576]{1,0:T(8,128)(2,1)} %pack.1.refs_6_), channel_id=1, source_target_pairs={{0,12},{4,8},{8,4},{12,0},{16,28},{20,24},{24,20},{28,16},{1,13},{... | collective-permute-start | bytes 411656 | tf_op jit(solution)/shard_map/ppermute | solution.py:178
  9.5 0.4 collective-permute-start.1
  10.0 0.5 %collective-permute-start = (bf16[8,8576]{1,0:T(8,128)(2,1)}, bf16[8,8576]{1,0:T(8,128)(2,1)S(1)}, u32[]{:S(2)}, u32[]{:S(2)}) collective-permute-start(bf16[8,8576]{1,0:T(8,128)(2,1)} %pack.1.refs_6_), channel_id=1, source_target_pairs={{0,4},{4,0},{8,12},{12,8},{16,20},{20,16},{24,28},{28,24},{1,5},{5... | collective-permute-start | bytes 411656 | tf_op jit(solution)/shard_map/ppermute | solution.py:178
  10.5 3.4 %collective-permute-done.3.refs_10_ = bf16[8,8576]{1,0:T(8,128)(2,1)S(1)} collective-permute-done((bf16[8,8576]{1,0:T(8,128)(2,1)}, bf16[8,8576]{1,0:T(8,128)(2,1)S(1)}, u32[]{:S(2)}, u32[]{:S(2)}) %collective-permute-start.3) | collective-permute-done | bytes 137248 | tf_op jit(solution)/shard_map/ppermute | solution.py:178
  13.9 1.7 %collective-permute-start.6 = (bf16[8,8576]{1,0:T(8,128)(2,1)S(1)}, bf16[8,8576]{1,0:T(8,128)(2,1)S(1)}, u32[]{:S(2)}, u32[]{:S(2)}) collective-permute-start(bf16[8,8576]{1,0:T(8,128)(2,1)S(1)} %collective-permute-done.3.refs_10_), channel_id=1, source_target_pairs={{0,12},{4,8},{8,4},{12,0},{16,28},{20,24},{24,20},{28,16},{1,13},{... | collective-permute-start | bytes 411656 | tf_op jit(solution)/shard_map/ppermute | solution.py:178
  15.6 1.3 %collective-permute-start.5 = (bf16[8,8576]{1,0:T(8,128)(2,1)S(1)}, bf16[8,8576]{1,0:T(8,128)(2,1)S(1)}, u32[]{:S(2)}, u32[]{:S(2)}) collective-permute-start(bf16[8,8576]{1,0:T(8,128)(2,1)S(1)} %collective-permute-done.3.refs_10_), channel_id=1, source_target_pairs={{0,8},{4,12},{8,0},{12,4},{16,24},{20,28},{24,16},{28,20},{1,9},{5... | collective-permute-start | bytes 411656 | tf_op jit(solution)/shard_map/ppermute | solution.py:178
  16.9 0.6 %collective-permute-start.4 = (bf16[8,8576]{1,0:T(8,128)(2,1)S(1)}, bf16[8,8576]{1,0:T(8,128)(2,1)S(1)}, u32[]{:S(2)}, u32[]{:S(2)}) collective-permute-start(bf16[8,8576]{1,0:T(8,128)(2,1)S(1)} %collective-permute-done.3.refs_10_), channel_id=1, source_target_pairs={{0,4},{4,0},{8,12},{12,8},{16,20},{20,16},{24,28},{28,24},{1,5},{5... | collective-permute-start | bytes 411656 | tf_op jit(solution)/shard_map/ppermute | solution.py:178
  17.5 1.3 %reshape.35.refs_3_ = f32[1,4224]{1,0:T(1,128)} reshape(f32[4224]{0:T(1024)} %param.9) | data formatting | bytes 33792 | tf_op jit(solution)/shard_map/reshape | solution.py:215
  18.9 6.2 %power.1.refs_5_ = bf16[432,4224]{1,0:T(8,128)(2,1)} custom-call(bf16[432,8448]{1,0:T(8,128)(2,1)} %refs_4_.1), custom_call_target="tpu_custom_call" | custom-call | tf_op jit(solution)/shard_map/power/pallas_call | solution.py:195
  25.2 0.6 %copy-done.2 = bf16[8,8576]{1,0:T(8,128)(2,1)} copy-done((bf16[8,8576]{1,0:T(8,128)(2,1)}, bf16[8,8576]{1,0:T(8,128)(2,1)S(1)}, u32[]{:S(2)}) %copy-start.2) | copy-done | bytes 137240
  26.0 8.6 %score.1 = (f32[432,64]{1,0:T(8,128)}, f32[4,64]{1,0:T(4,128)}) custom-call(s32[1]{0:T(128)} %bitcast.refs_0_, s32[1,64]{1,0:T(1,128)} %bitcast.7, s32[1,64]{1,0:T(1,128)} %bitcast.9, f32[1,4224]{1,0:T(1,128)} %reshape.35.refs_3_, bf16[432,8448]{1,0:T(8,128)(2,1)} %refs_4_.1, bf16[432,4224]{1,0:T(8,128)(2,1)} %power.1.refs_5_, bf16[8,8576]{1,0:T(8,128)(2,1)} %pack.1.refs_6_, ...), custom_call_target="tpu_custom_call" | custom-call | tf_op jit(solution)/shard_map/score/pallas_call | solution.py:203
  34.6 1.4 %collective-permute-start.7 = (f32[4,64]{1,0:T(4,128)}, f32[4,64]{1,0:T(4,128)S(1)}, u32[]{:S(2)}, u32[]{:S(2)}) collective-permute-start(f32[4,64]{1,0:T(4,128)} %get-tuple-element.12.stats), channel_id=1, source_target_pairs={{0,4},{4,0},{8,12},{12,8},{16,20},{20,16},{24,28},{28,24},{1,5},{5... | collective-permute-start | bytes 3080 | tf_op jit(solution)/shard_map/ppermute | solution.py:178
  36.0 2.4 %collective-permute-done.7 = f32[4,64]{1,0:T(4,128)S(1)} collective-permute-done((f32[4,64]{1,0:T(4,128)}, f32[4,64]{1,0:T(4,128)S(1)}, u32[]{:S(2)}, u32[]{:S(2)}) %collective-permute-start.7) | collective-permute-done | bytes 1056 | tf_op jit(solution)/shard_map/ppermute | solution.py:178
  38.4 0.7 %pad_maximum_fusion.1 = f32[8,64]{1,0:T(8,128)S(1)} fusion(f32[4,64]{1,0:T(4,128)S(1)} %collective-permute-done.7, f32[4,64]{1,0:T(4,128)} %get-tuple-element.12.stats), kind=kLoop, calls=%fused_computation.1 | loop fusion | flops 512 | bytes 4096 | tf_op jit(solution)/shard_map/concatenate | solution.py:220
  39.1 0.6 %collective-permute-start.8 = (f32[8,64]{1,0:T(8,128)S(1)}, f32[8,64]{1,0:T(8,128)S(1)}, u32[]{:S(2)}, u32[]{:S(2)}) collective-permute-start(f32[8,64]{1,0:T(8,128)S(1)} %pad_maximum_fusion.1), channel_id=1, source_target_pairs={{0,8},{4,12},{8,0},{12,4},{16,24},{20,28},{24,16},{28,20},{1,9},{5... | collective-permute-start | bytes 6152 | tf_op jit(solution)/shard_map/ppermute | solution.py:178
  39.7 3.0 %collective-permute-done.8 = f32[8,64]{1,0:T(8,128)S(1)} collective-permute-done((f32[8,64]{1,0:T(8,128)S(1)}, f32[8,64]{1,0:T(8,128)S(1)}, u32[]{:S(2)}, u32[]{:S(2)}) %collective-permute-start.8) | collective-permute-done | bytes 2080 | tf_op jit(solution)/shard_map/ppermute | solution.py:178
  42.7 0.7 %pad_maximum_fusion.refs_1_ = f32[16,64]{1,0:T(8,128)S(1)} fusion(f32[8,64]{1,0:T(8,128)S(1)} %collective-permute-done.8, f32[4,64]{1,0:T(4,128)S(1)} %collective-permute-done.7, f32[4,64]{1,0:T(4,128)} %get-tuple-element.12.stats), kind=kLoop, calls=%fused_computation | loop fusion | flops 2048 | bytes 8192 | tf_op jit(solution)/shard_map/concatenate | solution.py:220
  43.4 2.1 %collective-permute-start.9 = (f32[16,64]{1,0:T(8,128)S(1)}, f32[16,64]{1,0:T(8,128)S(1)}, u32[]{:S(2)}, u32[]{:S(2)}) collective-permute-start(f32[16,64]{1,0:T(8,128)S(1)} %pad_maximum_fusion.refs_1_), channel_id=1, source_target_pairs={{0,16},{4,20},{8,24},{12,28},{16,0},{20,4},{24,8},{28,12},{1,17},{... | collective-permute-start | bytes 12296 | tf_op jit(solution)/shard_map/ppermute | solution.py:178
  45.4 1.9 %running.1 = (f32[64,432]{1,0:T(8,128)}, f32[64,432]{1,0:T(8,128)}) custom-call(f32[432,64]{1,0:T(8,128)} %get-tuple-element.13.scores, f32[4,64]{1,0:T(4,128)} %get-tuple-element.12.stats), custom_call_target="tpu_custom_call" | custom-call | tf_op jit(solution)/shard_map/running/pallas_call | solution.py:226
  47.3 0.7 %collective-permute-done.9.refs_2_ = f32[16,64]{1,0:T(8,128)S(1)} collective-permute-done((f32[16,64]{1,0:T(8,128)S(1)}, f32[16,64]{1,0:T(8,128)S(1)}, u32[]{:S(2)}, u32[]{:S(2)}) %collective-permute-start.9) | collective-permute-done | bytes 4128 | tf_op jit(solution)/shard_map/ppermute | solution.py:178
  48.0 0.6 %copy-done.8 = f32[16,64]{1,0:T(8,128)} copy-done((f32[16,64]{1,0:T(8,128)}, f32[16,64]{1,0:T(8,128)S(1)}, u32[]{:S(2)}) %copy-start.8) | copy-done | bytes 4120
  48.6 1.9 %final.1 = (f32[64,432]{1,0:T(8,128)}, f32[64,432]{1,0:T(8,128)}, f32[1,64]{1,0:T(1,128)}, f32[1,64]{1,0:T(1,128)}) custom-call(s32[1]{0:T(128)} %bitcast.refs_0_, f32[16,64]{1,0:T(8,128)} %copy-done.7, f32[16,64]{1,0:T(8,128)} %copy-done.8, s32[1,64]{1,0:T(1,128)} %bitcast.12, s32[1,64]{1,0:T(1,128)} %bitcast.8, s32[1,64]{1,0:T(1,128)} %bitcast.10, ...), custom_call_target="tpu_custom_call" | custom-call | tf_op jit(solution)/shard_map/final/pallas_call | solution.py:235
  (22 shorter events, 0.2 us)
Async XLA Ops:
  2.9 11.0 %collective-permute-start.3 = (bf16[8,8576]{1,0:T(8,128)(2,1)}, bf16[8,8576]{1,0:T(8,128)(2,1)S(1)}, u32[]{:S(2)}, u32[]{:S(2)}) collective-permute-start(bf16[8,8576]{1,0:T(8,128)(2,1)} %pack.1.refs_6_), channel_id=1, source_target_pairs={{0,16},{4,20},{8,24},{12,28},{16,0},{20,4},{24,8},{28,12},{1,17},{... | collective-permute-start | bytes 411656 | tf_op jit(solution)/shard_map/ppermute | solution.py:178
  7.0 9.9 %collective-permute-start.2 = (bf16[8,8576]{1,0:T(8,128)(2,1)}, bf16[8,8576]{1,0:T(8,128)(2,1)S(1)}, u32[]{:S(2)}, u32[]{:S(2)}) collective-permute-start(bf16[8,8576]{1,0:T(8,128)(2,1)} %pack.1.refs_6_), channel_id=1, source_target_pairs={{0,12},{4,8},{8,4},{12,0},{16,28},{20,24},{24,20},{28,16},{1,13},{... | collective-permute-start | bytes 411656 | tf_op jit(solution)/shard_map/ppermute | solution.py:178
  9.5 15.6 %collective-permute-start.1 = (bf16[8,8576]{1,0:T(8,128)(2,1)}, bf16[8,8576]{1,0:T(8,128)(2,1)S(1)}, u32[]{:S(2)}, u32[]{:S(2)}) collective-permute-start(bf16[8,8576]{1,0:T(8,128)(2,1)} %pack.1.refs_6_), channel_id=1, source_target_pairs={{0,8},{4,12},{8,0},{12,4},{16,24},{20,28},{24,16},{28,20},{1,9},{5... | collective-permute-start | bytes 411656 | tf_op jit(solution)/shard_map/ppermute | solution.py:178
  10.0 15.1 %collective-permute-start = (bf16[8,8576]{1,0:T(8,128)(2,1)}, bf16[8,8576]{1,0:T(8,128)(2,1)S(1)}, u32[]{:S(2)}, u32[]{:S(2)}) collective-permute-start(bf16[8,8576]{1,0:T(8,128)(2,1)} %pack.1.refs_6_), channel_id=1, source_target_pairs={{0,4},{4,0},{8,12},{12,8},{16,20},{20,16},{24,28},{28,24},{1,5},{5... | collective-permute-start | bytes 411656 | tf_op jit(solution)/shard_map/ppermute | solution.py:178
  13.9 11.3 %copy-start = (bf16[8,8576]{1,0:T(8,128)(2,1)}, bf16[8,8576]{1,0:T(8,128)(2,1)S(1)}, u32[]{:S(2)}) copy-start(bf16[8,8576]{1,0:T(8,128)(2,1)S(1)} %collective-permute-done.3.refs_10_) | copy-start | bytes 411652
  13.9 11.3 %collective-permute-start.6 = (bf16[8,8576]{1,0:T(8,128)(2,1)S(1)}, bf16[8,8576]{1,0:T(8,128)(2,1)S(1)}, u32[]{:S(2)}, u32[]{:S(2)}) collective-permute-start(bf16[8,8576]{1,0:T(8,128)(2,1)S(1)} %collective-permute-done.3.refs_10_), channel_id=1, source_target_pairs={{0,12},{4,8},{8,4},{12,0},{16,28},{20,24},{24,20},{28,16},{1,13},{... | collective-permute-start | bytes 411656 | tf_op jit(solution)/shard_map/ppermute | solution.py:178
  15.6 9.6 %collective-permute-start.5 = (bf16[8,8576]{1,0:T(8,128)(2,1)S(1)}, bf16[8,8576]{1,0:T(8,128)(2,1)S(1)}, u32[]{:S(2)}, u32[]{:S(2)}) collective-permute-start(bf16[8,8576]{1,0:T(8,128)(2,1)S(1)} %collective-permute-done.3.refs_10_), channel_id=1, source_target_pairs={{0,8},{4,12},{8,0},{12,4},{16,24},{20,28},{24,16},{28,20},{1,9},{5... | collective-permute-start | bytes 411656 | tf_op jit(solution)/shard_map/ppermute | solution.py:178
  16.9 8.3 %copy-start.1 = (bf16[8,8576]{1,0:T(8,128)(2,1)}, bf16[8,8576]{1,0:T(8,128)(2,1)S(1)}, u32[]{:S(2)}) copy-start(bf16[8,8576]{1,0:T(8,128)(2,1)S(1)} %collective-permute-done.2.refs_9_) | copy-start | bytes 411652
  16.9 8.3 %collective-permute-start.4 = (bf16[8,8576]{1,0:T(8,128)(2,1)S(1)}, bf16[8,8576]{1,0:T(8,128)(2,1)S(1)}, u32[]{:S(2)}, u32[]{:S(2)}) collective-permute-start(bf16[8,8576]{1,0:T(8,128)(2,1)S(1)} %collective-permute-done.3.refs_10_), channel_id=1, source_target_pairs={{0,4},{4,0},{8,12},{12,8},{16,20},{20,16},{24,28},{28,24},{1,5},{5... | collective-permute-start | bytes 411656 | tf_op jit(solution)/shard_map/ppermute | solution.py:178
  25.1 0.7 %copy-start.2 = (bf16[8,8576]{1,0:T(8,128)(2,1)}, bf16[8,8576]{1,0:T(8,128)(2,1)S(1)}, u32[]{:S(2)}) copy-start(bf16[8,8576]{1,0:T(8,128)(2,1)S(1)} %collective-permute-done.1.refs_8_) | copy-start | bytes 411652
  25.1 0.7 %copy-start.3 = (bf16[8,8576]{1,0:T(8,128)(2,1)}, bf16[8,8576]{1,0:T(8,128)(2,1)S(1)}, u32[]{:S(2)}) copy-start(bf16[8,8576]{1,0:T(8,128)(2,1)S(1)} %collective-permute-done.refs_7_) | copy-start | bytes 411652
  25.1 0.7 %copy-start.4 = (bf16[8,8576]{1,0:T(8,128)(2,1)}, bf16[8,8576]{1,0:T(8,128)(2,1)S(1)}, u32[]{:S(2)}) copy-start(bf16[8,8576]{1,0:T(8,128)(2,1)S(1)} %collective-permute-done.6.refs_13_) | copy-start | bytes 411652
  25.2 0.8 %copy-start.5 = (bf16[8,8576]{1,0:T(8,128)(2,1)}, bf16[8,8576]{1,0:T(8,128)(2,1)S(1)}, u32[]{:S(2)}) copy-start(bf16[8,8576]{1,0:T(8,128)(2,1)S(1)} %collective-permute-done.5.refs_12_) | copy-start | bytes 411652
  25.2 0.8 %copy-start.6 = (bf16[8,8576]{1,0:T(8,128)(2,1)}, bf16[8,8576]{1,0:T(8,128)(2,1)S(1)}, u32[]{:S(2)}) copy-start(bf16[8,8576]{1,0:T(8,128)(2,1)S(1)} %collective-permute-done.4.refs_11_) | copy-start | bytes 411652
  34.6 3.8 %collective-permute-start.7 = (f32[4,64]{1,0:T(4,128)}, f32[4,64]{1,0:T(4,128)S(1)}, u32[]{:S(2)}, u32[]{:S(2)}) collective-permute-start(f32[4,64]{1,0:T(4,128)} %get-tuple-element.12.stats), channel_id=1, source_target_pairs={{0,4},{4,0},{8,12},{12,8},{16,20},{20,16},{24,28},{28,24},{1,5},{5... | collective-permute-start | bytes 3080 | tf_op jit(solution)/shard_map/ppermute | solution.py:178
  39.1 3.6 %collective-permute-start.8 = (f32[8,64]{1,0:T(8,128)S(1)}, f32[8,64]{1,0:T(8,128)S(1)}, u32[]{:S(2)}, u32[]{:S(2)}) collective-permute-start(f32[8,64]{1,0:T(8,128)S(1)} %pad_maximum_fusion.1), channel_id=1, source_target_pairs={{0,8},{4,12},{8,0},{12,4},{16,24},{20,28},{24,16},{28,20},{1,9},{5... | collective-permute-start | bytes 6152 | tf_op jit(solution)/shard_map/ppermute | solution.py:178
  43.3 4.6 %copy-start.7 = (f32[16,64]{1,0:T(8,128)}, f32[16,64]{1,0:T(8,128)S(1)}, u32[]{:S(2)}) copy-start(f32[16,64]{1,0:T(8,128)S(1)} %pad_maximum_fusion.refs_1_) | copy-start | bytes 12292
  43.4 4.6 %collective-permute-start.9 = (f32[16,64]{1,0:T(8,128)S(1)}, f32[16,64]{1,0:T(8,128)S(1)}, u32[]{:S(2)}, u32[]{:S(2)}) collective-permute-start(f32[16,64]{1,0:T(8,128)S(1)} %pad_maximum_fusion.refs_1_), channel_id=1, source_target_pairs={{0,16},{4,20},{8,24},{12,28},{16,0},{20,4},{24,8},{28,12},{1,17},{... | collective-permute-start | bytes 12296 | tf_op jit(solution)/shard_map/ppermute | solution.py:178
  48.0 0.6 %copy-start.8 = (f32[16,64]{1,0:T(8,128)}, f32[16,64]{1,0:T(8,128)S(1)}, u32[]{:S(2)}) copy-start(f32[16,64]{1,0:T(8,128)S(1)} %collective-permute-done.9.refs_2_) | copy-start | bytes 12292

commit v2 on v1

--- a/solution.py
+++ b/solution.py
@@ -10,7 +10,7 @@
 LANES = 128
 VMEM = pl.BlockSpec(memory_space=pltpu.VMEM)
 SMEM = pl.BlockSpec(memory_space=pltpu.SMEM)
-HBM = pl.BlockSpec(memory_space=pl.ANY)
+HBM = pl.BlockSpec(memory_space=pltpu.HBM)
 
 
 def sine(x):
@@ -35,11 +35,14 @@
     return jnp.sum(jnp.where(down == across, row, 0.0), axis=1, keepdims=True)
 
 
-def pack_body(particles, defocus, out, sem):
+def pack_body(particles, defocus, out, row, sems):
     feat = particles.shape[1]
-    copy = pltpu.make_async_copy(particles, out.at[:, pl.ds(0, feat)], sem)
+    copy = pltpu.make_async_copy(particles, out.at[:, pl.ds(0, feat)], sems.at[0])
+    fetch = pltpu.make_async_copy(defocus, row, sems.at[1])
     copy.start()
-    value = column(defocus[...])
+    fetch.start()
+    fetch.wait()
+    value = column(row[...])
     high = value.astype(jnp.bfloat16).astype(jnp.float32)
     mid = (value - high).astype(jnp.bfloat16).astype(jnp.float32)
     low = value - high - mid
@@ -49,45 +52,56 @@
     copy.wait()
 
 
-def power_body(references, out):
+def power_body(references, local, out, sems):
     rows, coef = out.shape
-    for k in range(0, coef, LANES):
-        real = references[:, pl.ds(k, LANES)].astype(jnp.float32)
-        imag = references[:, pl.ds(coef + k, LANES)].astype(jnp.float32)
-        out[:, pl.ds(k, LANES)] = (real * real + imag * imag).astype(jnp.bfloat16)
-
-
-def score_body(*refs, count, all_orients):
+    step = -(-rows // (8 * sems.shape[0])) * 8
+    spans = [pl.ds(r, min(step, rows - r)) for r in range(0, rows, step)]
+    copies = [pltpu.make_async_copy(references.at[span], local.at[span], sems.at[i]) for i, span in enumerate(spans)]
+    for copy in copies:
+        copy.start()
+    for span, copy in zip(spans, copies):
+        copy.wait()
+        for k in range(0, coef, LANES):
+            real = local[span, pl.ds(k, LANES)].astype(jnp.float32)
+            imag = local[span, pl.ds(coef + k, LANES)].astype(jnp.float32)
+            out[span, pl.ds(k, LANES)] = (real * real + imag * imag).astype(jnp.bfloat16)
+
+
+def score_body(*refs, pieces, all_orients):
     shard, start, length, noise, references, power = refs[:6]
-    pieces = refs[6 : 6 + count]
-    scores, stats = refs[6 + count : 8 + count]
-    stage, focus, weighted, energy = refs[8 + count :]
-    rows = pieces[0].shape[0]
+    packed = refs[6 : 6 + pieces]
+    scores, stats = refs[6 + pieces : 8 + pieces]
+    stage, focus, weighted, energy = refs[8 + pieces :]
+    rows = packed[0].shape[0]
+    count = focus.shape[0]
     ori, feat = references.shape
     coef = feat // 2
     me = shard[0]
-    places = [pl.ds(pl.multiple_of((me ^ b) * rows, rows), rows) for b in range(count)]
-    for b in range(count):
-        bits = pieces[b][:, pl.ds(feat, LANES)].astype(jnp.float32)
+    places = [pl.ds(pl.multiple_of((me ^ b) * rows, rows), rows) if pieces > 1 else pl.ds(0, rows) for b in range(pieces)]
+    for b in range(pieces):
+        bits = packed[b][:, pl.ds(feat, LANES)].astype(jnp.float32)
         value = bits[:, 0:1] + bits[:, 1:2] + bits[:, 2:3]
         focus[places[b], :] = jnp.broadcast_to(value, (rows, LANES))
     dims = (((1,), (1,)), ((), ()))
-    total = None
-    for first in range(0, coef, 2 * LANES):
-        width = min(2 * LANES, coef - first)
-        for k in range(first, first + width, LANES):
-            at = pl.ds(k, LANES)
-            also = pl.ds(coef + k, LANES)
-            for b in range(count):
-                stage[places[b], at] = pieces[b][:, at].astype(jnp.float32)
-                stage[places[b], also] = pieces[b][:, also].astype(jnp.float32)
-            row_pos = float(k // 128)
-            col_pos = (lax.broadcasted_iota(jnp.int32, (1, LANES), 1) - 64).astype(jnp.float32)
+    col_pos = (lax.broadcasted_iota(jnp.int32, (1, LANES), 1) - 64).astype(jnp.float32)
+
+    def images(at):
+        if pieces == 1:
+            return packed[0][:, at].astype(jnp.float32)
+        for b in range(pieces):
+            stage[places[b], at] = packed[b][:, at].astype(jnp.float32)
+        return stage[:, at]
+
+    def chunk(first, width, total):
+        for k in range(0, width, LANES):
+            at = pl.ds(first + k, LANES)
+            also = pl.ds(coef + first + k, LANES)
+            row_pos = jnp.asarray((first + k) // 128).astype(jnp.float32)
             freq = math.pi * (row_pos * row_pos + col_pos * col_pos) / 16384.0
             ctf = -sine(focus[...] * freq + 0.07)
-            noise_row = noise[:, at]
-            weighted[:, at] = (stage[:, at] * ctf * noise_row).astype(jnp.bfloat16)
-            weighted[:, also] = (stage[:, also] * ctf * noise_row).astype(jnp.bfloat16)
+            noise_row = noise[at].reshape(1, LANES)
+            weighted[:, at] = (images(at) * ctf * noise_row).astype(jnp.bfloat16)
+            weighted[:, also] = (images(also) * ctf * noise_row).astype(jnp.bfloat16)
             energy[:, at] = (-0.5 * (ctf * ctf * noise_row).astype(jnp.bfloat16).astype(jnp.float32)).astype(jnp.bfloat16)
         for left, right, k in (
             (references, weighted, first),
@@ -95,8 +109,24 @@
             (power, energy, first),
         ):
             at = pl.ds(k, width)
-            part = lax.dot_general(left[:, at], right[:, at], dims, preferred_element_type=jnp.float32)
-            total = part if total is None else total + part
+            total = total + lax.dot_general(left[:, at], right[:, at], dims, preferred_element_type=jnp.float32)
+        return total
+
+    step = 2 * LANES
+    total = jnp.zeros((ori, count), jnp.float32)
+    if pieces > 1:
+        for first in range(0, coef - coef % step, step):
+            total = chunk(first, step, total)
+    else:
+        scores[...] = total
+
+        @pl.loop(0, coef // step)
+        def _(i):
+            scores[...] = chunk(pl.multiple_of(i * step, step), step, scores[...])
+
+        total = scores[...]
+    if coef % step:
+        total = chunk(coef - coef % step, coef % step, total)
     scores[...] = total
     top = jnp.max(total, axis=0, keepdims=True)
     expon = jnp.exp(total - top)
@@ -162,6 +192,19 @@
     cumulative[...] = running[...] * scale + shift
 
 
+def call(body, name, limit, **kwargs):
+    params = pltpu.CompilerParams(vmem_limit_bytes=limit)
+    return pl.pallas_call(body, name=name, compiler_params=params, **kwargs)
+
+
+def in_vmem(x):
+    return pltpu.with_memory_space_constraint(x, pltpu.VMEM)
+
+
+def in_hbm(x):
+    return pltpu.with_memory_space_constraint(x, pltpu.HBM)
+
+
 def on_device(particles, defocus, inv_noise, references, thresholds, range_start, range_len):
     n = lax.axis_size("orient")
     rows, feat = particles.shape
@@ -170,49 +213,59 @@
     count = n * rows
     all_orients = n * ori
     shard = lax.axis_index("orient").astype(jnp.int32).reshape(1)
-    start = range_start.reshape(1, count)
-    length = range_len.reshape(1, count)
+    start = in_vmem(range_start.reshape(1, count))
+    length = in_vmem(range_len.reshape(1, count))
+    fraction = in_vmem(thresholds.reshape(1, count))
     f32, bf16 = jnp.float32, jnp.bfloat16
 
     def swap(x, b):
         return lax.ppermute(x, "orient", [(i, i ^ b) for i in range(n)])
 
-    packed = pl.pallas_call(
+    packed = call(
         pack_body,
-        name="pack",
-        out_shape=jax.ShapeDtypeStruct((rows, feat + LANES), bf16),
-        in_specs=[HBM, VMEM],
+        "pack",
+        2**21,
+        out_shape=pltpu.VMEM((rows, feat + LANES), bf16),
+        in_specs=[HBM, HBM],
         out_specs=VMEM,
-        scratch_shapes=[pltpu.SemaphoreType.DMA],
-    )(particles, defocus.reshape(1, rows))
+        scratch_shapes=[pltpu.VMEM((1, rows), f32), pltpu.SemaphoreType.DMA((2,))],
+    )(in_hbm(particles), in_hbm(defocus.reshape(1, rows)))
 
     half = n // 2
-    pieces = {0: packed, half: swap(packed, half)}
-    for source in (0, half):
-        for b in range(half - 1, 0, -1):
-            pieces[source ^ b] = swap(pieces[source], b)
-
-    power = pl.pallas_call(
+    if n <= 8:
+        pieces = {0: packed, half: swap(packed, half)}
+        for source in (0, half):
+            for b in range(half - 1, 0, -1):
+                pieces[source ^ b] = swap(pieces[source], b)
+        pieces = [pieces[b] for b in range(n)]
+    else:
+        pieces = [lax.all_gather(packed, "orient", axis=0, tiled=True)]
+
+    local, power = call(
         power_body,
-        name="power",
-        out_shape=jax.ShapeDtypeStruct((ori, coef), bf16),
-        in_specs=[VMEM],
-        out_specs=VMEM,
-    )(references)
-
-    scores, stats = pl.pallas_call(
-        lambda *refs: score_body(*refs, count=n, all_orients=all_orients),
-        name="score",
-        out_shape=(jax.ShapeDtypeStruct((ori, count), f32), jax.ShapeDtypeStruct((4, count), f32)),
-        in_specs=[SMEM] + [VMEM] * (5 + n),
+        "power",
+        2**21,
+        out_shape=(pltpu.VMEM((ori, feat), bf16), pltpu.VMEM((ori, coef), bf16)),
+        in_specs=[HBM],
+        out_specs=(VMEM, VMEM),
+        scratch_shapes=[pltpu.SemaphoreType.DMA((9,))],
+    )(in_hbm(references))
+
+    room = 2**22 + 4 * count * (feat + LANES) + 3 * count * feat
+    scores, stats = call(
+        lambda *refs: score_body(*refs, pieces=len(pieces), all_orients=all_orients),
+        "score",
+        room,
+        out_shape=(pltpu.VMEM((ori, count), f32), pltpu.VMEM((4, count), f32)),
+        in_specs=[SMEM] + [VMEM] * (5 + len(pieces)),
         out_specs=(VMEM, VMEM),
         scratch_shapes=[
-            pltpu.VMEM((count, feat), f32),
+            pltpu.VMEM((count, feat) if len(pieces) > 1 else (8, LANES), f32),
             pltpu.VMEM((count, LANES), f32),
             pltpu.VMEM((count, feat), bf16),
             pltpu.VMEM((count, coef), bf16),
         ],
-    )(shard, start, length, inv_noise.reshape(1, coef), references, power, *[pieces[b] for b in range(n)])
+    )(shard, start, length, in_vmem(inv_noise), in_vmem(local), in_vmem(power), *[in_vmem(p) for p in pieces])
 
     near = stats
     b = 1
@@ -223,22 +276,24 @@
 
     pad_ori = -(-ori // LANES) * LANES
     pad_count = -(-count // LANES) * LANES
-    expon, running = pl.pallas_call(
+    expon, running = call(
         running_body,
-        name="running",
-        out_shape=(jax.ShapeDtypeStruct((count, ori), f32),) * 2,
+        "running",
+        2**23,
+        out_shape=(pltpu.VMEM((count, ori), f32),) * 2,
         in_specs=[VMEM, VMEM],
         out_specs=(VMEM, VMEM),
         scratch_shapes=[pltpu.VMEM((pad_ori, pad_count), f32)] * 2,
-    )(scores, stats)
-
-    posterior, cumulative, evidence, mass = pl.pallas_call(
+    )(in_vmem(scores), in_vmem(stats))
+
+    posterior, cumulative, evidence, mass = call(
         lambda *refs: final_body(*refs, all_orients=all_orients),
-        name="final",
+        "final",
+        2**23,
         out_shape=(jax.ShapeDtypeStruct((count, ori), f32),) * 2 + (jax.ShapeDtypeStruct((1, count), f32),) * 2,
         in_specs=[SMEM] + [VMEM] * 7,
         out_specs=(VMEM,) * 4,
-    )(shard, near, far, thresholds.reshape(1, count), start, length, expon, running)
+    )(shard, in_vmem(near), in_vmem(far), fraction, start, length, in_vmem(expon), in_vmem(running))
     return posterior, cumulative, evidence.reshape(count), mass.reshape(count)
 
 

time: 50.8 us -> 39 us (0.77)
  Pallas kernels: 20.8 us -> 9 us
  waiting for transfers between devices: 9.42 us -> 14.3 us
  local copies, waits for them, and re-layouts: 2.71 us -> 0.02 us
  other arithmetic: 1.38 us -> 0.02 us
  starting transfers between devices: 15.4 us -> 14.8 us
    pallas_call x5, Pallas kernels: 20.8 us -> 9 us  [the longest x1 3.67 us: on_device(): call(lambda *refs: score_body(*refs, pieces=len(pieces), all_orients=all_...]
    ppermute x10, waiting for transfers between devices: 9.42 us -> 14.3 us  [swap(): return lax.ppermute(x, 'orient', [(i, i ^ b) for i in range(n)])]
    concatenate x2, other arithmetic: 1.38 us -> 0.02 us  [on_device(): near = jnp.concatenate([near, swap(near, b)], axis=0)]
    unnamed x18 -> x8, local copies, waits for them, and re-layouts: 1.37 us -> 0.02 us
    reshape x1 -> x0, local copies, waits for them, and re-layouts: 1.34 us -> none  [on_device(): inv_noise.reshape(1, coef)]
    ppermute x10, starting transfers between devices: 15.4 us -> 14.8 us  [swap(): return lax.ppermute(x, 'orient', [(i, i ^ b) for i in range(n)])]
  transfers between devices with their start and end apart: 10 -> 10, of which waited for: 4 -> 6; matrix products, arithmetic and copies ran while one was open for 3% -> 0% of each run, Pallas kernels for 16% -> 9%
where the time goes in v2:
time: 39 us; the launch traced here: 38.9 us
  starting transfers between devices  14.8 us (38%)
  waiting for transfers between devices  14.3 us (37%)
  Pallas kernels  9 us (23%)
  between operations  0.73 us (2%)
    ppermute x10, starting transfers between devices, swap(): return lax.ppermute(x, 'orient', [(i, i ^ b) for i in range(n)])  14.8 us
    ppermute x10, waiting for transfers between devices, swap(): return lax.ppermute(x, 'orient', [(i, i ^ b) for i in range(n)])  14.3 us
    pallas_call x1, Pallas kernels, on_device(): call(lambda *refs: score_body(*refs, pieces=len(pieces), all_orients=all_...  3.67 us
    pallas_call x1, Pallas kernels, on_device(): call(power_body, 'power', 2 ** 21, out_shape=(pltpu.VMEM((ori, feat), bf1...  3.32 us
    pallas_call x1, Pallas kernels, on_device(): call(pack_body, 'pack', 2 ** 21, out_shape=pltpu.VMEM((rows, feat + LANES...  0.94 us
    pallas_call x1, Pallas kernels, on_device(): call(lambda *refs: final_body(*refs, all_orients=all_orients), 'final', 2...  0.83 us
  transfers between devices with their start and end apart: 10, of which 6 were waited for; matrix products, arithmetic and copies ran while one was open for 0% of the time, Pallas kernels for 9%

profile of v2, /device:TPU:0, one launch (start us, length us, event | category | flops | bytes accessed | tf_op | source)
XLA Modules:
  0.0 38.9 jit_solution(10767392552127170124)
XLA Ops:
  0.7 0.9 %pack.1.refs_6_ = bf16[8,8576]{1,0:T(8,128)(2,1)S(1)} custom-call(bf16[8,8448]{1,0:T(8,128)(2,1)} %particles.1, f32[1,8]{1,0:T(1,128)} %bitcast.12), custom_call_target="tpu_custom_call" | custom-call | tf_op jit(solution)/shard_map/pack/pallas_call | solution.py:224
  1.6 4.1 %collective-permute-start.3 = (bf16[8,8576]{1,0:T(8,128)(2,1)S(1)}, bf16[8,8576]{1,0:T(8,128)(2,1)S(1)}, u32[]{:S(2)}, u32[]{:S(2)}) collective-permute-start(bf16[8,8576]{1,0:T(8,128)(2,1)S(1)} %pack.1.refs_6_), channel_id=1, source_target_pairs={{0,16},{4,20},{8,24},{12,28},{16,0},{20,4},{24,8},{28,12},{1,17},{... | collective-permute-start | bytes 411656 | tf_op jit(solution)/shard_map/ppermute | solution.py:222
  5.7 2.5 %collective-permute-start.2 = (bf16[8,8576]{1,0:T(8,128)(2,1)S(1)}, bf16[8,8576]{1,0:T(8,128)(2,1)S(1)}, u32[]{:S(2)}, u32[]{:S(2)}) collective-permute-start(bf16[8,8576]{1,0:T(8,128)(2,1)S(1)} %pack.1.refs_6_), channel_id=1, source_target_pairs={{0,12},{4,8},{8,4},{12,0},{16,28},{20,24},{24,20},{28,16},{1,13},{... | collective-permute-start | bytes 411656 | tf_op jit(solution)/shard_map/ppermute | solution.py:222
  8.3 0.4 %collective-permute-start.1 = (bf16[8,8576]{1,0:T(8,128)(2,1)S(1)}, bf16[8,8576]{1,0:T(8,128)(2,1)S(1)}, u32[]{:S(2)}, u32[]{:S(2)}) collective-permute-start(bf16[8,8576]{1,0:T(8,128)(2,1)S(1)} %pack.1.refs_6_), channel_id=1, source_target_pairs={{0,8},{4,12},{8,0},{12,4},{16,24},{20,28},{24,16},{28,20},{1,9},{5... | collective-permute-start | bytes 411656 | tf_op jit(solution)/shard_map/ppermute | solution.py:222
  8.7 0.5 %collective-permute-start = (bf16[8,8576]{1,0:T(8,128)(2,1)S(1)}, bf16[8,8576]{1,0:T(8,128)(2,1)S(1)}, u32[]{:S(2)}, u32[]{:S(2)}) collective-permute-start(bf16[8,8576]{1,0:T(8,128)(2,1)S(1)} %pack.1.refs_6_), channel_id=1, source_target_pairs={{0,4},{4,0},{8,12},{12,8},{16,20},{20,16},{24,28},{28,24},{1,5},{5... | collective-permute-start | bytes 411656 | tf_op jit(solution)/shard_map/ppermute | solution.py:222
  9.2 3.2 %collective-permute-done.3.refs_10_ = bf16[8,8576]{1,0:T(8,128)(2,1)S(1)} collective-permute-done((bf16[8,8576]{1,0:T(8,128)(2,1)S(1)}, bf16[8,8576]{1,0:T(8,128)(2,1)S(1)}, u32[]{:S(2)}, u32[]{:S(2)}) %collective-permute-start.3) | collective-permute-done | bytes 137248 | tf_op jit(solution)/shard_map/ppermute | solution.py:222
  12.4 1.6 %collective-permute-start.6 = (bf16[8,8576]{1,0:T(8,128)(2,1)S(1)}, bf16[8,8576]{1,0:T(8,128)(2,1)S(1)}, u32[]{:S(2)}, u32[]{:S(2)}) collective-permute-start(bf16[8,8576]{1,0:T(8,128)(2,1)S(1)} %collective-permute-done.3.refs_10_), channel_id=1, source_target_pairs={{0,12},{4,8},{8,4},{12,0},{16,28},{20,24},{24,20},{28,16},{1,13},{... | collective-permute-start | bytes 411656 | tf_op jit(solution)/shard_map/ppermute | solution.py:222
  14.0 1.4 %collective-permute-start.5 = (bf16[8,8576]{1,0:T(8,128)(2,1)S(1)}, bf16[8,8576]{1,0:T(8,128)(2,1)S(1)}, u32[]{:S(2)}, u32[]{:S(2)}) collective-permute-start(bf16[8,8576]{1,0:T(8,128)(2,1)S(1)} %collective-permute-done.3.refs_10_), channel_id=1, source_target_pairs={{0,8},{4,12},{8,0},{12,4},{16,24},{20,28},{24,16},{28,20},{1,9},{5... | collective-permute-start | bytes 411656 | tf_op jit(solution)/shard_map/ppermute | solution.py:222
  15.4 0.6 %collective-permute-start.4 = (bf16[8,8576]{1,0:T(8,128)(2,1)S(1)}, bf16[8,8576]{1,0:T(8,128)(2,1)S(1)}, u32[]{:S(2)}, u32[]{:S(2)}) collective-permute-start(bf16[8,8576]{1,0:T(8,128)(2,1)S(1)} %collective-permute-done.3.refs_10_), channel_id=1, source_target_pairs={{0,4},{4,0},{8,12},{12,8},{16,20},{20,16},{24,28},{28,24},{1,5},{5... | collective-permute-start | bytes 411656 | tf_op jit(solution)/shard_map/ppermute | solution.py:222
  16.1 3.3 %power.1 = (bf16[432,8448]{1,0:T(8,128)(2,1)S(1)}, bf16[432,4224]{1,0:T(8,128)(2,1)S(1)}) custom-call(bf16[432,8448]{1,0:T(8,128)(2,1)} %references.1), custom_call_target="tpu_custom_call" | custom-call | tf_op jit(solution)/shard_map/power/pallas_call | solution.py:244
  19.4 0.0 copy-start.3
  19.4 0.0 collective-permute-done.1.refs_8_
  19.4 0.0 collective-permute-done.refs_7_
  19.4 1.4 %collective-permute-done.6.refs_13_ = bf16[8,8576]{1,0:T(8,128)(2,1)S(1)} collective-permute-done((bf16[8,8576]{1,0:T(8,128)(2,1)S(1)}, bf16[8,8576]{1,0:T(8,128)(2,1)S(1)}, u32[]{:S(2)}, u32[]{:S(2)}) %collective-permute-start.6) | collective-permute-done | bytes 137248 | tf_op jit(solution)/shard_map/ppermute | solution.py:222
  20.8 1.5 %collective-permute-done.5.refs_12_ = bf16[8,8576]{1,0:T(8,128)(2,1)S(1)} collective-permute-done((bf16[8,8576]{1,0:T(8,128)(2,1)S(1)}, bf16[8,8576]{1,0:T(8,128)(2,1)S(1)}, u32[]{:S(2)}, u32[]{:S(2)}) %collective-permute-start.5) | collective-permute-done | bytes 137248 | tf_op jit(solution)/shard_map/ppermute | solution.py:222
  22.4 3.7 %score.1 = (f32[432,64]{1,0:T(8,128)S(1)}, f32[4,64]{1,0:T(4,128)S(1)}) custom-call(s32[1]{0:T(128)} %bitcast.refs_0_, s32[1,64]{1,0:T(1,128)S(1)} %bitcast.7, s32[1,64]{1,0:T(1,128)S(1)} %bitcast.9, f32[4224]{0:T(1024)S(1)} %copy-done, bf16[432,8448]{1,0:T(8,128)(2,1)S(1)} %get-tuple-element.14.refs_4_, bf16[432,4224]{1,0:T(8,128)(2,1)S(1)} %get-tuple-element.15.refs_5_, ...), custom_call_target="tpu_custom_call" | custom-call | tf_op jit(solution)/shard_map/score/pallas_call | solution.py:255
  26.1 0.6 %collective-permute-start.7 = (f32[4,64]{1,0:T(4,128)S(1)}, f32[4,64]{1,0:T(4,128)S(1)}, u32[]{:S(2)}, u32[]{:S(2)}) collective-permute-start(f32[4,64]{1,0:T(4,128)S(1)} %get-tuple-element.16.stats), channel_id=1, source_target_pairs={{0,4},{4,0},{8,12},{12,8},{16,20},{20,16},{24,28},{28,24},{1,5},{5... | collective-permute-start | bytes 3080 | tf_op jit(solution)/shard_map/ppermute | solution.py:222
  26.7 3.0 %collective-permute-done.7 = f32[4,64]{1,0:T(4,128)S(1)} collective-permute-done((f32[4,64]{1,0:T(4,128)S(1)}, f32[4,64]{1,0:T(4,128)S(1)}, u32[]{:S(2)}, u32[]{:S(2)}) %collective-permute-start.7) | collective-permute-done | bytes 1056 | tf_op jit(solution)/shard_map/ppermute | solution.py:222
  29.7 1.1 %collective-permute-start.8 = (f32[8,64]{1,0:T(8,128)S(1)}, f32[8,64]{1,0:T(8,128)S(1)}, u32[]{:S(2)}, u32[]{:S(2)}) collective-permute-start(f32[8,64]{1,0:T(8,128)S(1)} %pad_maximum_fusion.1), channel_id=1, source_target_pairs={{0,8},{4,12},{8,0},{12,4},{16,24},{20,28},{24,16},{28,20},{1,9},{5... | collective-permute-start | bytes 6152 | tf_op jit(solution)/shard_map/ppermute | solution.py:222
  30.8 2.6 %collective-permute-done.8 = f32[8,64]{1,0:T(8,128)S(1)} collective-permute-done((f32[8,64]{1,0:T(8,128)S(1)}, f32[8,64]{1,0:T(8,128)S(1)}, u32[]{:S(2)}, u32[]{:S(2)}) %collective-permute-start.8) | collective-permute-done | bytes 2080 | tf_op jit(solution)/shard_map/ppermute | solution.py:222
  33.4 1.9 %collective-permute-start.9 = (f32[16,64]{1,0:T(8,128)S(1)}, f32[16,64]{1,0:T(8,128)S(1)}, u32[]{:S(2)}, u32[]{:S(2)}) collective-permute-start(f32[16,64]{1,0:T(8,128)S(1)} %pad_maximum_fusion.refs_1_), channel_id=1, source_target_pairs={{0,16},{4,20},{8,24},{12,28},{16,0},{20,4},{24,8},{28,12},{1,17},{... | collective-permute-start | bytes 12296 | tf_op jit(solution)/shard_map/ppermute | solution.py:222
  35.3 0.2 running.1
  35.5 2.5 %collective-permute-done.9.refs_2_ = f32[16,64]{1,0:T(8,128)S(1)} collective-permute-done((f32[16,64]{1,0:T(8,128)S(1)}, f32[16,64]{1,0:T(8,128)S(1)}, u32[]{:S(2)}, u32[]{:S(2)}) %collective-permute-start.9) | collective-permute-done | bytes 4128 | tf_op jit(solution)/shard_map/ppermute | solution.py:222
  38.0 0.8 %final.1 = (f32[64,432]{1,0:T(8,128)}, f32[64,432]{1,0:T(8,128)}, f32[1,64]{1,0:T(1,128)}, f32[1,64]{1,0:T(1,128)}) custom-call(s32[1]{0:T(128)} %bitcast.refs_0_, f32[16,64]{1,0:T(8,128)S(1)} %pad_maximum_fusion.refs_1_, f32[16,64]{1,0:T(8,128)S(1)} %collective-permute-done.9.refs_2_, s32[1,64]{1,0:T(1,128)S(1)} %bitcast.11, s32[1,64]{1,0:T(1,128)S(1)} %bitcast.8, ...), custom_call_target="tpu_custom_call" | custom-call | tf_op jit(solution)/shard_map/final/pallas_call | solution.py:289
  (11 shorter events, 0.0 us)
Async XLA Ops:
  0.6 21.8 %copy-start.2 = (s32[64]{0:T(128)S(1)}, s32[64]{0:T(128)}, u32[]{:S(2)}) copy-start(s32[64]{0:T(128)} %param.13) | copy-start | bytes 772
  0.6 21.8 %copy-start.1 = (s32[64]{0:T(128)S(1)}, s32[64]{0:T(128)}, u32[]{:S(2)}) copy-start(s32[64]{0:T(128)} %param.12) | copy-start | bytes 772
  0.7 21.7 %copy-start = (f32[4224]{0:T(1024)S(1)}, f32[4224]{0:T(1024)}, u32[]{:S(2)}) copy-start(f32[4224]{0:T(1024)} %refs_3_.1) | copy-start | bytes 50692
  1.6 10.8 %collective-permute-start.3 = (bf16[8,8576]{1,0:T(8,128)(2,1)S(1)}, bf16[8,8576]{1,0:T(8,128)(2,1)S(1)}, u32[]{:S(2)}, u32[]{:S(2)}) collective-permute-start(bf16[8,8576]{1,0:T(8,128)(2,1)S(1)} %pack.1.refs_6_), channel_id=1, source_target_pairs={{0,16},{4,20},{8,24},{12,28},{16,0},{20,4},{24,8},{28,12},{1,17},{... | collective-permute-start | bytes 411656 | tf_op jit(solution)/shard_map/ppermute | solution.py:222
  5.7 9.7 %collective-permute-start.2 = (bf16[8,8576]{1,0:T(8,128)(2,1)S(1)}, bf16[8,8576]{1,0:T(8,128)(2,1)S(1)}, u32[]{:S(2)}, u32[]{:S(2)}) collective-permute-start(bf16[8,8576]{1,0:T(8,128)(2,1)S(1)} %pack.1.refs_6_), channel_id=1, source_target_pairs={{0,12},{4,8},{8,4},{12,0},{16,28},{20,24},{24,20},{28,16},{1,13},{... | collective-permute-start | bytes 411656 | tf_op jit(solution)/shard_map/ppermute | solution.py:222
  8.3 11.1 %collective-permute-start.1 = (bf16[8,8576]{1,0:T(8,128)(2,1)S(1)}, bf16[8,8576]{1,0:T(8,128)(2,1)S(1)}, u32[]{:S(2)}, u32[]{:S(2)}) collective-permute-start(bf16[8,8576]{1,0:T(8,128)(2,1)S(1)} %pack.1.refs_6_), channel_id=1, source_target_pairs={{0,8},{4,12},{8,0},{12,4},{16,24},{20,28},{24,16},{28,20},{1,9},{5... | collective-permute-start | bytes 411656 | tf_op jit(solution)/shard_map/ppermute | solution.py:222
  8.7 10.7 %collective-permute-start = (bf16[8,8576]{1,0:T(8,128)(2,1)S(1)}, bf16[8,8576]{1,0:T(8,128)(2,1)S(1)}, u32[]{:S(2)}, u32[]{:S(2)}) collective-permute-start(bf16[8,8576]{1,0:T(8,128)(2,1)S(1)} %pack.1.refs_6_), channel_id=1, source_target_pairs={{0,4},{4,0},{8,12},{12,8},{16,20},{20,16},{24,28},{28,24},{1,5},{5... | collective-permute-start | bytes 411656 | tf_op jit(solution)/shard_map/ppermute | solution.py:222
  12.4 8.4 %collective-permute-start.6 = (bf16[8,8576]{1,0:T(8,128)(2,1)S(1)}, bf16[8,8576]{1,0:T(8,128)(2,1)S(1)}, u32[]{:S(2)}, u32[]{:S(2)}) collective-permute-start(bf16[8,8576]{1,0:T(8,128)(2,1)S(1)} %collective-permute-done.3.refs_10_), channel_id=1, source_target_pairs={{0,12},{4,8},{8,4},{12,0},{16,28},{20,24},{24,20},{28,16},{1,13},{... | collective-permute-start | bytes 411656 | tf_op jit(solution)/shard_map/ppermute | solution.py:222
  14.0 8.3 %collective-permute-start.5 = (bf16[8,8576]{1,0:T(8,128)(2,1)S(1)}, bf16[8,8576]{1,0:T(8,128)(2,1)S(1)}, u32[]{:S(2)}, u32[]{:S(2)}) collective-permute-start(bf16[8,8576]{1,0:T(8,128)(2,1)S(1)} %collective-permute-done.3.refs_10_), channel_id=1, source_target_pairs={{0,8},{4,12},{8,0},{12,4},{16,24},{20,28},{24,16},{28,20},{1,9},{5... | collective-permute-start | bytes 411656 | tf_op jit(solution)/shard_map/ppermute | solution.py:222
  15.4 6.9 %collective-permute-start.4 = (bf16[8,8576]{1,0:T(8,128)(2,1)S(1)}, bf16[8,8576]{1,0:T(8,128)(2,1)S(1)}, u32[]{:S(2)}, u32[]{:S(2)}) collective-permute-start(bf16[8,8576]{1,0:T(8,128)(2,1)S(1)} %collective-permute-done.3.refs_10_), channel_id=1, source_target_pairs={{0,4},{4,0},{8,12},{12,8},{16,20},{20,16},{24,28},{28,24},{1,5},{5... | collective-permute-start | bytes 411656 | tf_op jit(solution)/shard_map/ppermute | solution.py:222
  19.4 18.6 %copy-start.3 = (s32[64]{0:T(128)S(1)}, s32[64]{0:T(128)}, u32[]{:S(2)}) copy-start(s32[64]{0:T(128)} %param.11) | copy-start | bytes 772
  26.1 3.6 %collective-permute-start.7 = (f32[4,64]{1,0:T(4,128)S(1)}, f32[4,64]{1,0:T(4,128)S(1)}, u32[]{:S(2)}, u32[]{:S(2)}) collective-permute-start(f32[4,64]{1,0:T(4,128)S(1)} %get-tuple-element.16.stats), channel_id=1, source_target_pairs={{0,4},{4,0},{8,12},{12,8},{16,20},{20,16},{24,28},{28,24},{1,5},{5... | collective-permute-start | bytes 3080 | tf_op jit(solution)/shard_map/ppermute | solution.py:222
  29.7 3.7 %collective-permute-start.8 = (f32[8,64]{1,0:T(8,128)S(1)}, f32[8,64]{1,0:T(8,128)S(1)}, u32[]{:S(2)}, u32[]{:S(2)}) collective-permute-start(f32[8,64]{1,0:T(8,128)S(1)} %pad_maximum_fusion.1), channel_id=1, source_target_pairs={{0,8},{4,12},{8,0},{12,4},{16,24},{20,28},{24,16},{28,20},{1,9},{5... | collective-permute-start | bytes 6152 | tf_op jit(solution)/shard_map/ppermute | solution.py:222
  33.4 4.6 %collective-permute-start.9 = (f32[16,64]{1,0:T(8,128)S(1)}, f32[16,64]{1,0:T(8,128)S(1)}, u32[]{:S(2)}, u32[]{:S(2)}) collective-permute-start(f32[16,64]{1,0:T(8,128)S(1)} %pad_maximum_fusion.refs_1_), channel_id=1, source_target_pairs={{0,16},{4,20},{8,24},{12,28},{16,0},{20,4},{24,8},{28,12},{1,17},{... | collective-permute-start | bytes 12296 | tf_op jit(solution)/shard_map/ppermute | solution.py:222

commit v3 on v2

--- a/solution.py
+++ b/solution.py
@@ -7,9 +7,10 @@
 from jax.experimental.pallas import tpu as pltpu
 from jax.sharding import PartitionSpec as P
 
+
 LANES = 128
+ROUTE = ((0, 4, 4), (0, 3, 3), (0, 2, 2), (0, 1, 1), (1, 3, 3), (1, 2, 2), (1, 1, 1))
 VMEM = pl.BlockSpec(memory_space=pltpu.VMEM)
-SMEM = pl.BlockSpec(memory_space=pltpu.SMEM)
 HBM = pl.BlockSpec(memory_space=pltpu.HBM)
 
 
@@ -67,17 +68,21 @@
             out[span, pl.ds(k, LANES)] = (real * real + imag * imag).astype(jnp.bfloat16)
 
 
-def score_body(*refs, pieces, all_orients):
-    shard, start, length, noise, references, power = refs[:6]
-    packed = refs[6 : 6 + pieces]
-    scores, stats = refs[6 + pieces : 8 + pieces]
-    stage, focus, weighted, energy = refs[8 + pieces :]
+def score_body(*refs, pieces, offsets, all_orients):
+    start, length, noise, references, power = refs[:5]
+    packed = refs[5 : 5 + pieces]
+    scores, stats = refs[5 + pieces : 7 + pieces]
+    stage, focus, weighted, energy = refs[7 + pieces :]
     rows = packed[0].shape[0]
     count = focus.shape[0]
     ori, feat = references.shape
     coef = feat // 2
-    me = shard[0]
-    places = [pl.ds(pl.multiple_of((me ^ b) * rows, rows), rows) if pieces > 1 else pl.ds(0, rows) for b in range(pieces)]
+    me = lax.axis_index("orient")
+    side = lax.axis_index("dom") & 1
+    places = [pl.ds(0, rows)]
+    if pieces > 1:
+        owners = [me ^ (even + side * (odd - even)) if even != odd else me ^ even for even, odd in offsets]
+        places = [pl.ds(pl.multiple_of(owner * rows, rows), rows) for owner in owners]
     for b in range(pieces):
         bits = packed[b][:, pl.ds(feat, LANES)].astype(jnp.float32)
         value = bits[:, 0:1] + bits[:, 1:2] + bits[:, 2:3]
@@ -163,9 +168,9 @@
                 out[pl.ds(c, high), pl.ds(o, width)] = block[:high, :width]
 
 
-def final_body(shard, near, far, thresholds, start, length, expon, running, *outs, all_orients):
+def final_body(near, far, thresholds, start, length, expon, running, *outs, all_orients):
     posterior, cumulative, evidence, mass = outs
-    me = shard[0]
+    me = lax.axis_index("orient")
     half = near.shape[0] // 4
     tables = [near[pl.ds(4 * b, 4), :] for b in range(half)] + [far[pl.ds(4 * b, 4), :] for b in range(half)]
     top = tables[0][0:1, :]
@@ -192,9 +197,9 @@
     cumulative[...] = running[...] * scale + shift
 
 
-def call(body, name, limit, **kwargs):
+def call(body, limit, **kwargs):
     params = pltpu.CompilerParams(vmem_limit_bytes=limit)
-    return pl.pallas_call(body, name=name, compiler_params=params, **kwargs)
+    return pl.pallas_call(body, compiler_params=params, **kwargs)
 
 
 def in_vmem(x):
@@ -212,18 +217,19 @@
     ori = references.shape[0]
     count = n * rows
     all_orients = n * ori
-    shard = lax.axis_index("orient").astype(jnp.int32).reshape(1)
     start = in_vmem(range_start.reshape(1, count))
     length = in_vmem(range_len.reshape(1, count))
     fraction = in_vmem(thresholds.reshape(1, count))
     f32, bf16 = jnp.float32, jnp.bfloat16
 
-    def swap(x, b):
-        return lax.ppermute(x, "orient", [(i, i ^ b) for i in range(n)])
+    def swap(x, even, odd):
+        steps = (even, odd)
+        parts = lax.axis_size("dom")
+        pairs = [(i * parts + d, (i ^ steps[d % 2]) * parts + d) for i in range(n) for d in range(parts)]
+        return lax.ppermute(x, ("orient", "dom"), pairs)
 
     packed = call(
         pack_body,
-        "pack",
         2**21,
         out_shape=pltpu.VMEM((rows, feat + LANES), bf16),
         in_specs=[HBM, HBM],
@@ -232,18 +238,17 @@
     )(in_hbm(particles), in_hbm(defocus.reshape(1, rows)))
 
     half = n // 2
-    if n <= 8:
-        pieces = {0: packed, half: swap(packed, half)}
-        for source in (0, half):
-            for b in range(half - 1, 0, -1):
-                pieces[source ^ b] = swap(pieces[source], b)
-        pieces = [pieces[b] for b in range(n)]
+    offsets = [(0, 0)]
+    if n == 8:
+        pieces = [packed]
+        for source, even, odd in ROUTE:
+            pieces.append(swap(pieces[source], even, odd))
+            offsets.append((offsets[source][0] ^ even, offsets[source][1] ^ odd))
     else:
         pieces = [lax.all_gather(packed, "orient", axis=0, tiled=True)]
 
     local, power = call(
         power_body,
-        "power",
         2**21,
         out_shape=(pltpu.VMEM((ori, feat), bf16), pltpu.VMEM((ori, coef), bf16)),
         in_specs=[HBM],
@@ -253,11 +258,10 @@
 
     room = 2**22 + 4 * count * (feat + LANES) + 3 * count * feat
     scores, stats = call(
-        lambda *refs: score_body(*refs, pieces=len(pieces), all_orients=all_orients),
-        "score",
+        lambda *refs: score_body(*refs, pieces=len(pieces), offsets=offsets, all_orients=all_orients),
         room,
         out_shape=(pltpu.VMEM((ori, count), f32), pltpu.VMEM((4, count), f32)),
-        in_specs=[SMEM] + [VMEM] * (5 + len(pieces)),
+        in_specs=[VMEM] * (5 + len(pieces)),
         out_specs=(VMEM, VMEM),
         scratch_shapes=[
             pltpu.VMEM((count, feat) if len(pieces) > 1 else (8, LANES), f32),
@@ -265,20 +269,22 @@
             pltpu.VMEM((count, feat), bf16),
             pltpu.VMEM((count, coef), bf16),
         ],
-    )(shard, start, length, in_vmem(inv_noise), in_vmem(local), in_vmem(power), *[in_vmem(p) for p in pieces])
-
-    near = stats
-    b = 1
-    while b < half:
-        near = jnp.concatenate([near, swap(near, b)], axis=0)
-        b *= 2
-    far = swap(near, half)
+    )(start, length, in_vmem(inv_noise), in_vmem(local), in_vmem(power), *[in_vmem(p) for p in pieces])
+
+    if n == 8:
+        near = jnp.concatenate([stats] + [swap(stats, b, b) for b in range(1, half)], axis=0)
+    else:
+        near = stats
+        b = 1
+        while b < half:
+            near = jnp.concatenate([near, swap(near, b, b)], axis=0)
+            b *= 2
+    far = swap(near, half, half)
 
     pad_ori = -(-ori // LANES) * LANES
     pad_count = -(-count // LANES) * LANES
     expon, running = call(
         running_body,
-        "running",
         2**23,
         out_shape=(pltpu.VMEM((count, ori), f32),) * 2,
         in_specs=[VMEM, VMEM],
@@ -288,12 +294,11 @@
 
     posterior, cumulative, evidence, mass = call(
         lambda *refs: final_body(*refs, all_orients=all_orients),
-        "final",
         2**23,
         out_shape=(jax.ShapeDtypeStruct((count, ori), f32),) * 2 + (jax.ShapeDtypeStruct((1, count), f32),) * 2,
-        in_specs=[SMEM] + [VMEM] * 7,
+        in_specs=[VMEM] * 7,
         out_specs=(VMEM,) * 4,
-    )(shard, in_vmem(near), in_vmem(far), fraction, start, length, in_vmem(expon), in_vmem(running))
+    )(in_vmem(near), in_vmem(far), fraction, start, length, in_vmem(expon), in_vmem(running))
     return posterior, cumulative, evidence.reshape(count), mass.reshape(count)
 
 

time: 39 us -> 38.6 us (0.990)
  waiting for transfers between devices: 14.3 us -> 12.1 us
  starting transfers between devices: 14.8 us -> 16.6 us
    ppermute x10 -> x11, waiting for transfers between devices: 14.3 us -> 12.1 us  [swap(): return lax.ppermute(x, ('orient', 'dom'), pairs)]
    ppermute x10 -> x11, starting transfers between devices: 14.8 us -> 16.6 us  [swap(): return lax.ppermute(x, ('orient', 'dom'), pairs)]
  transfers between devices with their start and end apart: 10 -> 11, of which waited for: 6 -> 8; matrix products, arithmetic and copies ran while one was open for 0% -> 0% of each run, Pallas kernels for 9% -> 9%
where the time goes in v3:
time: 38.6 us; the launch traced here: 38.5 us
  starting transfers between devices  16.6 us (43%)
  waiting for transfers between devices  12.1 us (31%)
  Pallas kernels  9.09 us (24%)
  between operations  0.72 us (2%)
    ppermute x11, starting transfers between devices, swap(): return lax.ppermute(x, ('orient', 'dom'), pairs)  16.6 us
    ppermute x11, waiting for transfers between devices, swap(): return lax.ppermute(x, ('orient', 'dom'), pairs)  12.1 us
    pallas_call x1, Pallas kernels, on_device(): call(lambda *refs: score_body(*refs, pieces=len(pieces), offsets=offsets,...  3.75 us
    pallas_call x1, Pallas kernels, on_device(): call(power_body, 2 ** 21, out_shape=(pltpu.VMEM((ori, feat), bf16), pltpu...  3.32 us
    pallas_call x1, Pallas kernels, on_device(): call(pack_body, 2 ** 21, out_shape=pltpu.VMEM((rows, feat + LANES), bf16)...  0.94 us
    pallas_call x1, Pallas kernels, on_device(): call(lambda *refs: final_body(*refs, all_orients=all_orients), 2 ** 23, o...  0.83 us
  transfers between devices with their start and end apart: 11, of which 8 were waited for; matrix products, arithmetic and copies ran while one was open for 0% of the time, Pallas kernels for 9%

profile of v3, /device:TPU:0, one launch (start us, length us, event | category | flops | bytes accessed | tf_op | source)
XLA Modules:
  0.0 38.5 jit_solution(7766521995378964032)
XLA Ops:
  0.7 0.9 %shard_map.103.refs_5_ = bf16[8,8576]{1,0:T(8,128)(2,1)S(1)} custom-call(bf16[8,8448]{1,0:T(8,128)(2,1)} %particles.1, f32[1,8]{1,0:T(1,128)} %bitcast.11), custom_call_target="tpu_custom_call" | custom-call | tf_op jit(solution)/shard_map/pallas_call | solution.py:231
  1.6 4.1 %collective-permute-start = (bf16[8,8576]{1,0:T(8,128)(2,1)S(1)}, bf16[8,8576]{1,0:T(8,128)(2,1)S(1)}, u32[]{:S(2)}, u32[]{:S(2)}) collective-permute-start(bf16[8,8576]{1,0:T(8,128)(2,1)S(1)} %shard_map.103.refs_5_), channel_id=1, source_target_pairs={{0,16},{1,17},{2,18},{3,19},{4,20},{5,21},{6,22},{7,23},{8,24},{9,... | collective-permute-start | bytes 411656 | tf_op jit(solution)/shard_map/ppermute | solution.py:229
  5.7 1.5 %collective-permute-start.3 = (bf16[8,8576]{1,0:T(8,128)(2,1)S(1)}, bf16[8,8576]{1,0:T(8,128)(2,1)S(1)}, u32[]{:S(2)}, u32[]{:S(2)}) collective-permute-start(bf16[8,8576]{1,0:T(8,128)(2,1)S(1)} %shard_map.103.refs_5_), channel_id=1, source_target_pairs={{0,4},{1,5},{2,6},{3,7},{4,0},{5,1},{6,2},{7,3},{8,12},{9,13},{10,... | collective-permute-start | bytes 411656 | tf_op jit(solution)/shard_map/ppermute | solution.py:229
  7.3 1.6 %collective-permute-start.2 = (bf16[8,8576]{1,0:T(8,128)(2,1)S(1)}, bf16[8,8576]{1,0:T(8,128)(2,1)S(1)}, u32[]{:S(2)}, u32[]{:S(2)}) collective-permute-start(bf16[8,8576]{1,0:T(8,128)(2,1)S(1)} %shard_map.103.refs_5_), channel_id=1, source_target_pairs={{0,8},{1,9},{2,10},{3,11},{4,12},{5,13},{6,14},{7,15},{8,0},{9,1},... | collective-permute-start | bytes 411656 | tf_op jit(solution)/shard_map/ppermute | solution.py:229
  8.8 0.4 %collective-permute-start.1 = (bf16[8,8576]{1,0:T(8,128)(2,1)S(1)}, bf16[8,8576]{1,0:T(8,128)(2,1)S(1)}, u32[]{:S(2)}, u32[]{:S(2)}) collective-permute-start(bf16[8,8576]{1,0:T(8,128)(2,1)S(1)} %shard_map.103.refs_5_), channel_id=1, source_target_pairs={{0,12},{1,13},{2,14},{3,15},{4,8},{5,9},{6,10},{7,11},{8,4},{9,5},... | collective-permute-start | bytes 411656 | tf_op jit(solution)/shard_map/ppermute | solution.py:229
  9.2 3.2 %collective-permute-done.refs_6_ = bf16[8,8576]{1,0:T(8,128)(2,1)S(1)} collective-permute-done((bf16[8,8576]{1,0:T(8,128)(2,1)S(1)}, bf16[8,8576]{1,0:T(8,128)(2,1)S(1)}, u32[]{:S(2)}, u32[]{:S(2)}) %collective-permute-start) | collective-permute-done | bytes 137248 | tf_op jit(solution)/shard_map/ppermute | solution.py:229
  12.4 1.6 %collective-permute-start.6 = (bf16[8,8576]{1,0:T(8,128)(2,1)S(1)}, bf16[8,8576]{1,0:T(8,128)(2,1)S(1)}, u32[]{:S(2)}, u32[]{:S(2)}) collective-permute-start(bf16[8,8576]{1,0:T(8,128)(2,1)S(1)} %collective-permute-done.refs_6_), channel_id=1, source_target_pairs={{0,4},{1,5},{2,6},{3,7},{4,0},{5,1},{6,2},{7,3},{8,12},{9,13},{10,... | collective-permute-start | bytes 411656 | tf_op jit(solution)/shard_map/ppermute | solution.py:229
  14.0 0.6 %collective-permute-start.5 = (bf16[8,8576]{1,0:T(8,128)(2,1)S(1)}, bf16[8,8576]{1,0:T(8,128)(2,1)S(1)}, u32[]{:S(2)}, u32[]{:S(2)}) collective-permute-start(bf16[8,8576]{1,0:T(8,128)(2,1)S(1)} %collective-permute-done.refs_6_), channel_id=1, source_target_pairs={{0,8},{1,9},{2,10},{3,11},{4,12},{5,13},{6,14},{7,15},{8,0},{9,1},... | collective-permute-start | bytes 411656 | tf_op jit(solution)/shard_map/ppermute | solution.py:229
  14.6 1.3 %collective-permute-start.4 = (bf16[8,8576]{1,0:T(8,128)(2,1)S(1)}, bf16[8,8576]{1,0:T(8,128)(2,1)S(1)}, u32[]{:S(2)}, u32[]{:S(2)}) collective-permute-start(bf16[8,8576]{1,0:T(8,128)(2,1)S(1)} %collective-permute-done.refs_6_), channel_id=1, source_target_pairs={{0,12},{1,13},{2,14},{3,15},{4,8},{5,9},{6,10},{7,11},{8,4},{9,5},... | collective-permute-start | bytes 411656 | tf_op jit(solution)/shard_map/ppermute | solution.py:229
  15.9 3.3 %shard_map.102 = (bf16[432,8448]{1,0:T(8,128)(2,1)S(1)}, bf16[432,4224]{1,0:T(8,128)(2,1)S(1)}) custom-call(bf16[432,8448]{1,0:T(8,128)(2,1)} %references.1), custom_call_target="tpu_custom_call" | custom-call | tf_op jit(solution)/shard_map/pallas_call | solution.py:250
  19.3 0.7 %collective-permute-done.6.refs_12_ = bf16[8,8576]{1,0:T(8,128)(2,1)S(1)} collective-permute-done((bf16[8,8576]{1,0:T(8,128)(2,1)S(1)}, bf16[8,8576]{1,0:T(8,128)(2,1)S(1)}, u32[]{:S(2)}, u32[]{:S(2)}) %collective-permute-start.6) | collective-permute-done | bytes 137248 | tf_op jit(solution)/shard_map/ppermute | solution.py:229
  19.9 0.8 %collective-permute-done.5.refs_11_ = bf16[8,8576]{1,0:T(8,128)(2,1)S(1)} collective-permute-done((bf16[8,8576]{1,0:T(8,128)(2,1)S(1)}, bf16[8,8576]{1,0:T(8,128)(2,1)S(1)}, u32[]{:S(2)}, u32[]{:S(2)}) %collective-permute-start.5) | collective-permute-done | bytes 137248 | tf_op jit(solution)/shard_map/ppermute | solution.py:229
  20.8 2.0 %collective-permute-done.4.refs_10_ = bf16[8,8576]{1,0:T(8,128)(2,1)S(1)} collective-permute-done((bf16[8,8576]{1,0:T(8,128)(2,1)S(1)}, bf16[8,8576]{1,0:T(8,128)(2,1)S(1)}, u32[]{:S(2)}, u32[]{:S(2)}) %collective-permute-start.4) | collective-permute-done | bytes 137248 | tf_op jit(solution)/shard_map/ppermute | solution.py:229
  22.7 3.8 %shard_map.104 = (f32[432,64]{1,0:T(8,128)S(1)}, f32[4,64]{1,0:T(4,128)S(1)}) custom-call(s32[1,64]{1,0:T(1,128)S(1)} %bitcast.6, s32[1,64]{1,0:T(1,128)S(1)} %bitcast.8, f32[4224]{0:T(1024)S(1)} %copy-done, bf16[432,8448]{1,0:T(8,128)(2,1)S(1)} %get-tuple-element.14.refs_3_, bf16[432,4224]{1,0:T(8,128)(2,1)S(1)} %get-tuple-element.15.refs_4_, ...), custom_call_target="tpu_custom_call" | custom-call | tf_op jit(solution)/shard_map/pallas_call | solution.py:260
  26.5 1.1 %collective-permute-start.9 = (f32[4,64]{1,0:T(4,128)S(1)}, f32[4,64]{1,0:T(4,128)S(1)}, u32[]{:S(2)}, u32[]{:S(2)}) collective-permute-start(f32[4,64]{1,0:T(4,128)S(1)} %get-tuple-element.16.stats), channel_id=1, source_target_pairs={{0,12},{1,13},{2,14},{3,15},{4,8},{5,9},{6,10},{7,11},{8,4},{9,5},... | collective-permute-start | bytes 3080 | tf_op jit(solution)/shard_map/ppermute | solution.py:229
  27.6 1.8 %collective-permute-start.8 = (f32[4,64]{1,0:T(4,128)S(1)}, f32[4,64]{1,0:T(4,128)S(1)}, u32[]{:S(2)}, u32[]{:S(2)}) collective-permute-start(f32[4,64]{1,0:T(4,128)S(1)} %get-tuple-element.16.stats), channel_id=1, source_target_pairs={{0,8},{1,9},{2,10},{3,11},{4,12},{5,13},{6,14},{7,15},{8,0},{9,1},... | collective-permute-start | bytes 3080 | tf_op jit(solution)/shard_map/ppermute | solution.py:229
  29.4 0.6 %collective-permute-start.7 = (f32[4,64]{1,0:T(4,128)S(1)}, f32[4,64]{1,0:T(4,128)S(1)}, u32[]{:S(2)}, u32[]{:S(2)}) collective-permute-start(f32[4,64]{1,0:T(4,128)S(1)} %get-tuple-element.16.stats), channel_id=1, source_target_pairs={{0,4},{1,5},{2,6},{3,7},{4,0},{5,1},{6,2},{7,3},{8,12},{9,13},{10,... | collective-permute-start | bytes 3080 | tf_op jit(solution)/shard_map/ppermute | solution.py:229
  30.0 1.0 %collective-permute-done.9 = f32[4,64]{1,0:T(4,128)S(1)} collective-permute-done((f32[4,64]{1,0:T(4,128)S(1)}, f32[4,64]{1,0:T(4,128)S(1)}, u32[]{:S(2)}, u32[]{:S(2)}) %collective-permute-start.9) | collective-permute-done | bytes 1056 | tf_op jit(solution)/shard_map/ppermute | solution.py:229
  31.0 0.2 collective-permute-done.8
  31.2 1.8 %collective-permute-done.7 = f32[4,64]{1,0:T(4,128)S(1)} collective-permute-done((f32[4,64]{1,0:T(4,128)S(1)}, f32[4,64]{1,0:T(4,128)S(1)}, u32[]{:S(2)}, u32[]{:S(2)}) %collective-permute-start.7) | collective-permute-done | bytes 1056 | tf_op jit(solution)/shard_map/ppermute | solution.py:229
  33.0 1.9 %collective-permute-start.10 = (f32[16,64]{1,0:T(8,128)S(1)}, f32[16,64]{1,0:T(8,128)S(1)}, u32[]{:S(2)}, u32[]{:S(2)}) collective-permute-start(f32[16,64]{1,0:T(8,128)S(1)} %pad_maximum_fusion.refs_0_), channel_id=1, source_target_pairs={{0,16},{1,17},{2,18},{3,19},{4,20},{5,21},{6,22},{7,23},{8,24},{9,... | collective-permute-start | bytes 12296 | tf_op jit(solution)/shard_map/ppermute | solution.py:229
  34.9 0.2 shard_map.105
  35.2 2.5 %collective-permute-done.10.refs_1_ = f32[16,64]{1,0:T(8,128)S(1)} collective-permute-done((f32[16,64]{1,0:T(8,128)S(1)}, f32[16,64]{1,0:T(8,128)S(1)}, u32[]{:S(2)}, u32[]{:S(2)}) %collective-permute-start.10) | collective-permute-done | bytes 4128 | tf_op jit(solution)/shard_map/ppermute | solution.py:229
  37.6 0.8 %shard_map.106 = (f32[64,432]{1,0:T(8,128)}, f32[64,432]{1,0:T(8,128)}, f32[1,64]{1,0:T(1,128)}, f32[1,64]{1,0:T(1,128)}) custom-call(f32[16,64]{1,0:T(8,128)S(1)} %pad_maximum_fusion.refs_0_, f32[16,64]{1,0:T(8,128)S(1)} %collective-permute-done.10.refs_1_, s32[1,64]{1,0:T(1,128)S(1)} %bitcast.10, s32[1,64]{1,0:T(1,128)S(1)} %bitcast.7, ...), custom_call_target="tpu_custom_call" | custom-call | tf_op jit(solution)/shard_map/pallas_call | solution.py:295
  (12 shorter events, 0.0 us)
Async XLA Ops:
  0.6 22.1 %copy-start.2 = (s32[64]{0:T(128)S(1)}, s32[64]{0:T(128)}, u32[]{:S(2)}) copy-start(s32[64]{0:T(128)} %param.13) | copy-start | bytes 772
  0.6 22.1 %copy-start.1 = (s32[64]{0:T(128)S(1)}, s32[64]{0:T(128)}, u32[]{:S(2)}) copy-start(s32[64]{0:T(128)} %param.12) | copy-start | bytes 772
  0.7 22.1 %copy-start = (f32[4224]{0:T(1024)S(1)}, f32[4224]{0:T(1024)}, u32[]{:S(2)}) copy-start(f32[4224]{0:T(1024)} %refs_2_.1) | copy-start | bytes 50692
  1.6 10.8 %collective-permute-start = (bf16[8,8576]{1,0:T(8,128)(2,1)S(1)}, bf16[8,8576]{1,0:T(8,128)(2,1)S(1)}, u32[]{:S(2)}, u32[]{:S(2)}) collective-permute-start(bf16[8,8576]{1,0:T(8,128)(2,1)S(1)} %shard_map.103.refs_5_), channel_id=1, source_target_pairs={{0,16},{1,17},{2,18},{3,19},{4,20},{5,21},{6,22},{7,23},{8,24},{9,... | collective-permute-start | bytes 411656 | tf_op jit(solution)/shard_map/ppermute | solution.py:229
  5.7 8.9 %collective-permute-start.3 = (bf16[8,8576]{1,0:T(8,128)(2,1)S(1)}, bf16[8,8576]{1,0:T(8,128)(2,1)S(1)}, u32[]{:S(2)}, u32[]{:S(2)}) collective-permute-start(bf16[8,8576]{1,0:T(8,128)(2,1)S(1)} %shard_map.103.refs_5_), channel_id=1, source_target_pairs={{0,4},{1,5},{2,6},{3,7},{4,0},{5,1},{6,2},{7,3},{8,12},{9,13},{10,... | collective-permute-start | bytes 411656 | tf_op jit(solution)/shard_map/ppermute | solution.py:229
  7.3 12.0 %collective-permute-start.2 = (bf16[8,8576]{1,0:T(8,128)(2,1)S(1)}, bf16[8,8576]{1,0:T(8,128)(2,1)S(1)}, u32[]{:S(2)}, u32[]{:S(2)}) collective-permute-start(bf16[8,8576]{1,0:T(8,128)(2,1)S(1)} %shard_map.103.refs_5_), channel_id=1, source_target_pairs={{0,8},{1,9},{2,10},{3,11},{4,12},{5,13},{6,14},{7,15},{8,0},{9,1},... | collective-permute-start | bytes 411656 | tf_op jit(solution)/shard_map/ppermute | solution.py:229
  8.8 10.4 %collective-permute-start.1 = (bf16[8,8576]{1,0:T(8,128)(2,1)S(1)}, bf16[8,8576]{1,0:T(8,128)(2,1)S(1)}, u32[]{:S(2)}, u32[]{:S(2)}) collective-permute-start(bf16[8,8576]{1,0:T(8,128)(2,1)S(1)} %shard_map.103.refs_5_), channel_id=1, source_target_pairs={{0,12},{1,13},{2,14},{3,15},{4,8},{5,9},{6,10},{7,11},{8,4},{9,5},... | collective-permute-start | bytes 411656 | tf_op jit(solution)/shard_map/ppermute | solution.py:229
  12.4 7.5 %collective-permute-start.6 = (bf16[8,8576]{1,0:T(8,128)(2,1)S(1)}, bf16[8,8576]{1,0:T(8,128)(2,1)S(1)}, u32[]{:S(2)}, u32[]{:S(2)}) collective-permute-start(bf16[8,8576]{1,0:T(8,128)(2,1)S(1)} %collective-permute-done.refs_6_), channel_id=1, source_target_pairs={{0,4},{1,5},{2,6},{3,7},{4,0},{5,1},{6,2},{7,3},{8,12},{9,13},{10,... | collective-permute-start | bytes 411656 | tf_op jit(solution)/shard_map/ppermute | solution.py:229
  14.0 6.8 %collective-permute-start.5 = (bf16[8,8576]{1,0:T(8,128)(2,1)S(1)}, bf16[8,8576]{1,0:T(8,128)(2,1)S(1)}, u32[]{:S(2)}, u32[]{:S(2)}) collective-permute-start(bf16[8,8576]{1,0:T(8,128)(2,1)S(1)} %collective-permute-done.refs_6_), channel_id=1, source_target_pairs={{0,8},{1,9},{2,10},{3,11},{4,12},{5,13},{6,14},{7,15},{8,0},{9,1},... | collective-permute-start | bytes 411656 | tf_op jit(solution)/shard_map/ppermute | solution.py:229
  14.6 8.1 %collective-permute-start.4 = (bf16[8,8576]{1,0:T(8,128)(2,1)S(1)}, bf16[8,8576]{1,0:T(8,128)(2,1)S(1)}, u32[]{:S(2)}, u32[]{:S(2)}) collective-permute-start(bf16[8,8576]{1,0:T(8,128)(2,1)S(1)} %collective-permute-done.refs_6_), channel_id=1, source_target_pairs={{0,12},{1,13},{2,14},{3,15},{4,8},{5,9},{6,10},{7,11},{8,4},{9,5},... | collective-permute-start | bytes 411656 | tf_op jit(solution)/shard_map/ppermute | solution.py:229
  19.2 18.4 %copy-start.3 = (s32[64]{0:T(128)S(1)}, s32[64]{0:T(128)}, u32[]{:S(2)}) copy-start(s32[64]{0:T(128)} %param.11) | copy-start | bytes 772
  26.5 4.5 %collective-permute-start.9 = (f32[4,64]{1,0:T(4,128)S(1)}, f32[4,64]{1,0:T(4,128)S(1)}, u32[]{:S(2)}, u32[]{:S(2)}) collective-permute-start(f32[4,64]{1,0:T(4,128)S(1)} %get-tuple-element.16.stats), channel_id=1, source_target_pairs={{0,12},{1,13},{2,14},{3,15},{4,8},{5,9},{6,10},{7,11},{8,4},{9,5},... | collective-permute-start | bytes 3080 | tf_op jit(solution)/shard_map/ppermute | solution.py:229
  27.6 3.6 %collective-permute-start.8 = (f32[4,64]{1,0:T(4,128)S(1)}, f32[4,64]{1,0:T(4,128)S(1)}, u32[]{:S(2)}, u32[]{:S(2)}) collective-permute-start(f32[4,64]{1,0:T(4,128)S(1)} %get-tuple-element.16.stats), channel_id=1, source_target_pairs={{0,8},{1,9},{2,10},{3,11},{4,12},{5,13},{6,14},{7,15},{8,0},{9,1},... | collective-permute-start | bytes 3080 | tf_op jit(solution)/shard_map/ppermute | solution.py:229
  29.4 3.6 %collective-permute-start.7 = (f32[4,64]{1,0:T(4,128)S(1)}, f32[4,64]{1,0:T(4,128)S(1)}, u32[]{:S(2)}, u32[]{:S(2)}) collective-permute-start(f32[4,64]{1,0:T(4,128)S(1)} %get-tuple-element.16.stats), channel_id=1, source_target_pairs={{0,4},{1,5},{2,6},{3,7},{4,0},{5,1},{6,2},{7,3},{8,12},{9,13},{10,... | collective-permute-start | bytes 3080 | tf_op jit(solution)/shard_map/ppermute | solution.py:229
  33.0 4.6 %collective-permute-start.10 = (f32[16,64]{1,0:T(8,128)S(1)}, f32[16,64]{1,0:T(8,128)S(1)}, u32[]{:S(2)}, u32[]{:S(2)}) collective-permute-start(f32[16,64]{1,0:T(8,128)S(1)} %pad_maximum_fusion.refs_0_), channel_id=1, source_target_pairs={{0,16},{1,17},{2,18},{3,19},{4,20},{5,21},{6,22},{7,23},{8,24},{9,... | collective-permute-start | bytes 12296 | tf_op jit(solution)/shard_map/ppermute | solution.py:229
